TPU v7x, 256 devices: a whole 4x4x8 slice. The times are simulated.
256 devices in a mesh: grp: 8 (over x_lo, y), tp: 32 (over x_hi, z, core).
Axes of the slice: x: 4 (x_hi: 2, x_lo: 2; x = x_hi * 2 + x_lo), y: 4, z: 8, core: 2. Of those that a mesh axis runs over, the one named last changes fastest.
Arguments:
- batch_sizes: int32 [8], P('grp'), may hold values from 1 to 16
- seq_lens: int32 [8, 16], P('grp'), may hold values from 1 to 8192
- page_table: int32 [8, 16, 512], P('grp', None, 'tp'), may hold values from 0 to 255, as said below
- queries: bfloat16 [8, 16, 4096], P('grp', None, 'tp'), may hold values from -4 to 14
- kv_pool: bfloat16 [8, 8192, 16, 1024], P('grp', 'tp'), may hold values from -7 to 7
- new_kv: bfloat16 [8, 16, 1024], P('grp'), may hold values from -6 to 6
- out_weight: bfloat16 [4096, 2880], P('tp', 'grp'), may hold values from -0.375 to 0.375
Outputs:
- mixed: float32 [8, 16, 2880], P('grp')
Inputs may be any that keep to these rules, and one draw needn't show every extreme that they name: `batch_sizes`: slots below a group's batch size are live; the others are empty and their outputs are zero. `seq_lens`: entries of empty slots are drawn but unused. `page_table`: for every group g and every t, the entries [g, :, t * 16 to (t + 1) * 16 - 1] are a permutation of 0 to 255.
All inputs are finite; a program needn't handle non-finite values.
Results may differ from a plain program's by a relative error of at most 0.007.
Values may be sent and summed in bfloat16 or wider, within the bound.
No kernel may reach another device: no remote copies, remote signals or barrier semaphores. Data moves between devices by JAX's collectives and lax.ppermute only.
A program may use at most 64 MiB of HBM per device.

v0:
```python
import functools

import jax
import jax.numpy as jnp
from jax import lax
from jax.experimental import pallas as pl
from jax.experimental.pallas import tpu as pltpu
from jax.sharding import PartitionSpec as P


HEADS = 64
KV_HEADS = 8
HD = 64
LANES = 128
NEG_BIG = -1e30
BF = jnp.bfloat16
F32 = jnp.float32
STAT_ROW = 16
MSG_ROWS = 24
INTERPRET = False
STEPS = (4, 1, 2, 3)
UNROLL = 2
AHEAD = 2


def lane_iota(rows):
    return lax.broadcasted_iota(jnp.int32, (rows, LANES), 1)


def roll_lanes(x, shift):
    return pltpu.roll(x, shift, 1)


def split_bf(x):
    hi = x.astype(BF)
    lo = (x - hi.astype(F32)).astype(BF)
    return hi, lo


def attend_kernel(
    info_ref, lens_ref, table_ref, q_ref, pool_ref, out_ref, kv_scr, q_scr, num_scr, stat_scr, sems
):
    n_tp, slots, _ = q_ref.shape
    pages = table_ref.shape[1]
    page_len = pool_ref.shape[1]
    kv_cols = KV_HEADS * HD
    tokens = pages * page_len
    live_count = info_ref[0]
    tp_index = info_ref[1]
    steps = (live_count + UNROLL - 1) // UNROLL

    def load_pages(slot):
        for i in range(pages):
            pltpu.make_async_copy(
                pool_ref.at[table_ref[slot, i]], kv_scr.at[slot, i], sems.at[slot]
            ).start()

    def wait_pages(slot):
        pltpu.make_async_copy(
            pool_ref.at[pl.ds(0, pages)], kv_scr.at[slot], sems.at[slot]
        ).wait()

    for step in range(AHEAD):

        @pl.when(step < steps)
        def _():
            for i in range(UNROLL):
                load_pages(step * UNROLL + i)

    q_scr[...] = (q_ref[...].astype(F32) * HD**-0.5).reshape(n_tp * slots, LANES)
    num_scr[...] = jnp.zeros_like(num_scr)
    low_half = lane_iota(n_tp) < HD
    own_block = (
        lax.broadcasted_iota(jnp.int32, (n_tp, kv_cols), 1) // HD
        == lax.broadcasted_iota(jnp.int32, (n_tp, kv_cols), 0) // (n_tp // KV_HEADS)
    )
    column = lax.broadcasted_iota(jnp.int32, (HEADS, tokens), 1)
    position = (column // page_len) * (page_len * n_tp) + tp_index * page_len + column % page_len
    lane = lane_iota(HEADS)

    def slot_queries(slot):
        x = q_scr[pl.ds(slot, n_tp, stride=slots), :]
        turned = roll_lanes(x, HD)
        even = jnp.where(low_half, x, turned)
        odd = jnp.where(low_half, turned, x)
        wide = [jnp.where(own_block, jnp.concatenate([h] * 4, axis=1), 0.0) for h in (even, odd)]
        return jnp.concatenate(wide, axis=0).astype(BF)

    def slot_scores(slot):
        keys = kv_scr[slot, :, :, 0:kv_cols].reshape(tokens, kv_cols)
        return lax.dot_general(
            slot_queries(slot), keys, (((1,), (1,)), ((), ())), preferred_element_type=F32
        )

    def slot_weights(slot, scores):
        live = position < jnp.where(slot < live_count, lens_ref[slot], 0)
        scores = jnp.where(live, scores, NEG_BIG)
        top = jnp.max(scores, axis=1, keepdims=True)
        top = (top + jnp.abs(top) * 2.0**-7).astype(BF).astype(F32)
        weights = jnp.where(live, jnp.exp(scores - top), 0.0)
        return top, jnp.sum(weights, axis=1, keepdims=True), weights.astype(BF)

    def slot_values(slot, weights):
        values = kv_scr[slot, :, :, kv_cols : 2 * kv_cols].reshape(tokens, kv_cols)
        mixed = jnp.dot(weights, values, preferred_element_type=F32)
        folded = []
        for part in (mixed[:n_tp], mixed[n_tp:]):
            part = jnp.where(own_block, part, 0.0)
            part = sum(part[:, i * LANES : (i + 1) * LANES] for i in range(4))
            folded.append(part + roll_lanes(part, HD))
        num_scr[pl.ds(pl.multiple_of(slot * n_tp, n_tp), n_tp), :] = jnp.where(
            low_half, folded[0], folded[1]
        )

    def some_slots(step, state):
        tops, sums = state
        group = [step * UNROLL + i for i in range(UNROLL)]

        @pl.when(step + AHEAD < steps)
        def _():
            for slot in group:
                load_pages(slot + AHEAD * UNROLL)

        for slot in group:
            wait_pages(slot)
        scores = [slot_scores(slot) for slot in group]
        parts = [slot_weights(slot, s) for slot, s in zip(group, scores)]
        for slot, (top, total, weights) in zip(group, parts):
            slot_values(slot, weights)
            here = lane == slot
            tops = jnp.where(here, top, tops)
            sums = jnp.where(here, total, sums)
        return tops, sums

    start = (
        jnp.where(lane < slots, NEG_BIG, 0.0).astype(F32),
        jnp.zeros((HEADS, LANES), F32),
    )
    tops, sums = lax.fori_loop(0, steps, some_slots, start)
    hi, lo = split_bf(sums)
    packed = tops + roll_lanes(hi.astype(F32), slots) + roll_lanes(lo.astype(F32), 2 * slots)
    stat_scr[...] = packed[:n_tp] + roll_lanes(packed[n_tp:], HD)
    for t in range(n_tp):
        out_ref[t, 0:slots, :] = num_scr[pl.ds(t, slots, stride=n_tp), :].astype(BF)
        out_ref[t, STAT_ROW:MSG_ROWS, :] = jnp.broadcast_to(
            stat_scr[t : t + 1, :], (MSG_ROWS - STAT_ROW, LANES)
        ).astype(BF)


def combine_kernel(info_ref, msg_ref, q_ref, new_ref, *rest):
    pair_refs, out_ref = rest[:-1], rest[-1]
    n_tp = msg_ref.shape[0]
    slots = q_ref.shape[0]
    live_count = info_ref[0]
    tp_index = info_ref[1]
    grp_index = info_ref[2]
    blocks = 2 * len(pair_refs)
    width = pair_refs[0].shape[0] // 2
    ones_block = (
        lax.broadcasted_iota(jnp.int32, (LANES, LANES), 0) // HD
        == lax.broadcasted_iota(jnp.int32, (LANES, LANES), 1) // HD
    ).astype(F32).astype(BF)
    rows8 = MSG_ROWS - STAT_ROW
    stats = [msg_ref[t, STAT_ROW:MSG_ROWS, :].astype(F32) for t in range(n_tp)]
    top = functools.reduce(jnp.maximum, stats)
    scale = [jnp.exp(s - top) for s in stats]
    sums = sum(
        w * (roll_lanes(s, LANES - slots) + roll_lanes(s, LANES - 2 * slots))
        for w, s in zip(scale, stats)
    )
    sub = lax.broadcasted_iota(jnp.int32, (rows8, LANES), 0)
    within = lane_iota(rows8) % HD
    picks = [within == sub + rows8 * i for i in range(slots // rows8)]
    picked = jnp.concatenate(
        [jnp.where(p, v, 0.0) for v in (*scale, top, sums) for p in picks], axis=0
    )
    hi, lo = split_bf(picked)
    spread = jnp.dot(hi, ones_block, preferred_element_type=F32) + jnp.dot(
        lo, ones_block, preferred_element_type=F32
    )
    top_all = spread[n_tp * slots : (n_tp + 1) * slots]
    sum_all = spread[(n_tp + 1) * slots :]
    numerator = sum(
        msg_ref[t, 0:slots, :].astype(F32) * spread[t * slots : (t + 1) * slots]
        for t in range(n_tp)
    )

    kv_head = tp_index // (n_tp // KV_HEADS)
    low_half = lane_iota(slots) < HD

    def own_columns(first):
        at = pl.multiple_of(first + (kv_head // 2) * LANES, LANES)
        block = new_ref[:, pl.ds(at, LANES)].astype(F32)
        turned = roll_lanes(block, HD)
        low = jnp.where(low_half, block, turned)
        high = jnp.where(low_half, turned, block)
        return jnp.where(kv_head % 2 == 0, low, high)

    new_key = own_columns(0)
    new_value = own_columns(KV_HEADS * HD)
    products = q_ref[...].astype(F32) * HD**-0.5 * new_key
    hi, lo = split_bf(products)
    self_score = jnp.dot(hi, ones_block, preferred_element_type=F32) + jnp.dot(
        lo, ones_block, preferred_element_type=F32
    )
    final_top = jnp.maximum(top_all, self_score)
    cached = jnp.exp(top_all - final_top)
    fresh = jnp.exp(self_score - final_top)
    attended = (numerator * cached + new_value * fresh) / (sum_all * cached + fresh)
    slot = lax.broadcasted_iota(jnp.int32, (slots, LANES), 0)
    attended = jnp.where(slot < live_count, attended, 0.0).astype(BF)
    parts = n_tp // blocks
    rows = slots // parts
    for k in range(blocks):
        first = k % 2 * width
        share = lax.dot_general(
            attended,
            pair_refs[k // 2][first : first + width, :],
            (((1,), (1,)), ((), ())),
            preferred_element_type=F32,
        ).astype(BF)
        offset = (0, STEPS[0])[k % 2] ^ (0, *STEPS[1:])[k // 2]
        block = jnp.bitwise_xor(grp_index, offset)
        for i in range(parts):
            out_ref[block * parts + i, :, 0:width] = share[i * rows : (i + 1) * rows]


def copies_kernel(in_ref, out_ref):
    out_ref[...] = jnp.broadcast_to(in_ref[...][None], out_ref.shape)


def total_kernel(in_ref, out_ref):
    n_tp = in_ref.shape[0]
    total = sum(in_ref[t].astype(F32) for t in range(n_tp)).astype(BF)
    for t in range(n_tp):
        out_ref[t] = total


def finish_kernel(in_ref, out_ref):
    n_tp, rows, _ = in_ref.shape
    parts = out_ref.shape[1] // rows
    blocks = n_tp // parts
    width = out_ref.shape[2] // blocks
    for b in range(blocks):
        for i in range(parts):
            out_ref[0, i * rows : (i + 1) * rows, b * width : (b + 1) * width] = in_ref[
                b * parts + i, :, 0:width
            ].astype(F32)


SMEM = functools.partial(pl.BlockSpec, memory_space=pltpu.SMEM)
VMEM = functools.partial(pl.BlockSpec, memory_space=pltpu.VMEM)
PARAMS = pltpu.CompilerParams(vmem_limit_bytes=16 << 20)


def near(x):
    return x if INTERPRET else pltpu.with_memory_space_constraint(x, pltpu.VMEM)


def far(x):
    return x if INTERPRET else pltpu.with_memory_space_constraint(x, pltpu.HBM)


def near_out(shape, dtype):
    return jax.ShapeDtypeStruct(shape, dtype) if INTERPRET else pltpu.VMEM(shape, dtype)


def copies(piece, count):
    return pl.pallas_call(
        copies_kernel,
        out_shape=near_out((count, *piece.shape), piece.dtype),
        in_specs=[VMEM()],
        out_specs=VMEM(),
        interpret=INTERPRET,
        compiler_params=PARAMS,
        name="copies",
    )(far(piece))


def attend(info, lens, table, gathered, pool):
    n_tp, slots, _ = gathered.shape
    return pl.pallas_call(
        attend_kernel,
        out_shape=near_out((n_tp, MSG_ROWS, LANES), BF),
        in_specs=[SMEM(), SMEM(), SMEM(), VMEM(), pl.BlockSpec(memory_space=pltpu.HBM)],
        out_specs=VMEM(),
        scratch_shapes=[
            pltpu.VMEM((slots, table.shape[1], *pool.shape[1:]), BF),
            pltpu.VMEM((n_tp * slots, LANES), F32),
            pltpu.VMEM((slots * n_tp, LANES), F32),
            pltpu.VMEM((n_tp, LANES), F32),
            pltpu.SemaphoreType.DMA((slots,)),
        ],
        interpret=INTERPRET,
        compiler_params=PARAMS,
        name="attend",
    )(info, far(lens), far(table), near(gathered), far(pool))


def combine(info, message, own, fresh, pairs):
    n_tp = message.shape[0]
    slots = own.shape[0]
    rows = slots * 2 * len(pairs) // n_tp
    width = -(-pairs[0].shape[0] // 2 // LANES) * LANES
    return pl.pallas_call(
        combine_kernel,
        out_shape=near_out((n_tp, rows, width), BF),
        in_specs=[SMEM()] + [VMEM()] * (3 + len(pairs)),
        out_specs=VMEM(),
        interpret=INTERPRET,
        compiler_params=PARAMS,
        name="combine",
    )(info, near(message), near(own), near(fresh), *map(near, pairs))


def total_copies(pieces):
    return pl.pallas_call(
        total_kernel,
        out_shape=near_out(pieces.shape, BF),
        in_specs=[VMEM()],
        out_specs=VMEM(),
        interpret=INTERPRET,
        compiler_params=PARAMS,
        name="total",
    )(near(pieces))


def finish(pieces, slots, width):
    return pl.pallas_call(
        finish_kernel,
        out_shape=jax.ShapeDtypeStruct((1, slots, width), F32),
        in_specs=[VMEM()],
        out_specs=VMEM(),
        interpret=INTERPRET,
        compiler_params=PARAMS,
        name="finish",
    )(near(pieces))


def exchange(pieces, axis):
    return lax.all_to_all(pieces, axis, split_axis=0, concat_axis=0, tiled=True)


def local(batch_sizes, seq_lens, page_table, queries, kv_pool, new_kv, out_weight):
    n_tp = lax.axis_size("tp")
    n_grp = lax.axis_size("grp")
    tp_index = lax.axis_index("tp")
    grp_index = lax.axis_index("grp")
    own = queries[0]
    slots = own.shape[0]
    info = jnp.stack([batch_sizes[0], tp_index.astype(jnp.int32), grp_index.astype(jnp.int32)])

    def from_pair(blocks, step):
        return lax.ppermute(blocks, "grp", [(i, i ^ step) for i in range(n_grp)])

    own_block = out_weight.T
    pair = jnp.concatenate([own_block, from_pair(own_block, STEPS[0])])
    gathered = exchange(copies(own, n_tp), "tp")
    pair, gathered = lax.optimization_barrier((pair, gathered))
    pairs = [pair] + [from_pair(pair, step) for step in STEPS[1:]]
    message = attend(info, seq_lens[0], page_table[0], gathered, kv_pool[0])
    received = exchange(message, "tp")
    shares = combine(info, received, own, new_kv[0], pairs)
    totals = total_copies(exchange(shares, "tp"))
    return finish(exchange(totals, "tp"), slots, n_grp * out_weight.shape[1])


def solution(mesh):
    return jax.shard_map(
        local,
        mesh=mesh,
        in_specs=(
            P("grp"),
            P("grp", None),
            P("grp", None, "tp"),
            P("grp", None, "tp"),
            P("grp", "tp", None, None),
            P("grp", None, None),
            P("tp", "grp"),
        ),
        out_specs=P("grp", None, None),
        check_vma=False,
    )
```

profile of v0, /device:TPU:1, one launch (start us, length us, event | category | flops | bytes accessed | tf_op | source)
XLA Modules:
  0.0 86.6 jit_solution(12599225088735157377)
XLA Ops:
  0.0 0.0 copy-start.1
  0.0 0.0 copy-start
  0.0 1.4 %copies.1 = bf16[32,16,128]{2,1,0:T(8,128)(2,1)} custom-call(bf16[16,128]{1,0:T(8,128)(2,1)} %bitcast.9), custom_call_target="tpu_custom_call" | custom-call | tf_op jit(solution)/shard_map/copies/pallas_call | solution.py:269
  1.4 12.6 %all-to-all-start = ((bf16[32,16,128]{2,1,0:T(8,128)(2,1)}), bf16[32,16,128]{2,1,0:T(8,128)(2,1)S(1)}, u32[]{:S(2)}, u32[]{:S(2)}) async-start(bf16[32,16,128]{2,1,0:T(8,128)(2,1)} %copies.1), calls=%async_computation | async-start | bytes 262144 | tf_op jit(solution)/shard_map/all_to_all | solution.py:341
  14.0 0.4 collective-permute-start
  15.1 0.1 pad_add_fusion.info_ref
  15.1 3.6 %collective-permute-done = bf16[360,128]{1,0:T(8,128)(2,1)S(1)} collective-permute-done((bf16[360,128]{1,0:T(8,128)(2,1)}, bf16[360,128]{1,0:T(8,128)(2,1)S(1)}, u32[]{:S(2)}, u32[]{:S(2)}) %collective-permute-start) | collective-permute-done | bytes 92192 | tf_op jit(solution)/shard_map/ppermute | solution.py:354
  18.8 0.9 %pad_maximum_fusion.rest_0_ = bf16[720,128]{1,0:T(8,128)(2,1)S(1)} fusion(bf16[360,128]{1,0:T(8,128)(2,1)S(1)} %collective-permute-done, bf16[360,128]{1,0:T(8,128)(2,1)} %bitcast.13), kind=kLoop, calls=%fused_computation | loop fusion | flops 368640 | bytes 368640 | tf_op jit(solution)/shard_map/concatenate | solution.py:357
  19.7 4.8 %all-to-all-done.q_ref = bf16[32,16,128]{2,1,0:T(8,128)(2,1)S(1)} async-done(((bf16[32,16,128]{2,1,0:T(8,128)(2,1)}), bf16[32,16,128]{2,1,0:T(8,128)(2,1)S(1)}, u32[]{:S(2)}, u32[]{:S(2)}) %all-to-all-start) | async-done | bytes 131104 | tf_op jit(solution)/shard_map/all_to_all | solution.py:341
  24.5 4.3 %attend.1 = bf16[32,24,128]{2,1,0:T(8,128)(2,1)} custom-call(s32[3]{0:T(128)S(1)} %pad_add_fusion.info_ref, s32[16]{0:T(128)} %bitcast.15, s32[16,16]{1,0:T(8,128)} %bitcast.14, bf16[32,16,128]{2,1,0:T(8,128)(2,1)S(1)} %all-to-all-done.q_ref, bf16[256,16,1024]{2,1,0:T(8,128)(2,1)} %bitcast.11), custom_call_target="tpu_custom_call" | custom-call | tf_op jit(solution)/shard_map/attend/pallas_call | solution.py:282
  28.8 6.1 %all-to-all-start.1 = ((bf16[32,24,128]{2,1,0:T(8,128)(2,1)}), bf16[32,24,128]{2,1,0:T(8,128)(2,1)S(1)}, u32[]{:S(2)}, u32[]{:S(2)}) async-start(bf16[32,24,128]{2,1,0:T(8,128)(2,1)} %attend.1), calls=%async_computation.1 | async-start | bytes 393216 | tf_op jit(solution)/shard_map/all_to_all | solution.py:341
  34.9 3.4 %collective-permute-start.3 = (bf16[720,128]{1,0:T(8,128)(2,1)S(1)}, bf16[720,128]{1,0:T(8,128)(2,1)S(1)}, u32[]{:S(2)}, u32[]{:S(2)}) collective-permute-start(bf16[720,128]{1,0:T(8,128)(2,1)S(1)} %pad_maximum_fusion.rest_0_), channel_id=1, source_target_pairs={{0,96},{32,64},{64,32},{96,0},{128,224},{160,192},{192,160},{224,1... | collective-permute-start | bytes 552968 | tf_op jit(solution)/shard_map/ppermute | solution.py:354
  38.3 3.7 %collective-permute-start.2 = (bf16[720,128]{1,0:T(8,128)(2,1)S(1)}, bf16[720,128]{1,0:T(8,128)(2,1)S(1)}, u32[]{:S(2)}, u32[]{:S(2)}) collective-permute-start(bf16[720,128]{1,0:T(8,128)(2,1)S(1)} %pad_maximum_fusion.rest_0_), channel_id=1, source_target_pairs={{0,64},{32,96},{64,0},{96,32},{128,192},{160,224},{192,128},{224,1... | collective-permute-start | bytes 552968 | tf_op jit(solution)/shard_map/ppermute | solution.py:354
  42.0 0.0 collective-permute-start.1
  42.0 1.1 %collective-permute-done.3.rest_3_ = bf16[720,128]{1,0:T(8,128)(2,1)S(1)} collective-permute-done((bf16[720,128]{1,0:T(8,128)(2,1)S(1)}, bf16[720,128]{1,0:T(8,128)(2,1)S(1)}, u32[]{:S(2)}, u32[]{:S(2)}) %collective-permute-start.3) | collective-permute-done | bytes 184352 | tf_op jit(solution)/shard_map/ppermute | solution.py:354
  43.1 3.8 %collective-permute-done.2.rest_2_ = bf16[720,128]{1,0:T(8,128)(2,1)S(1)} collective-permute-done((bf16[720,128]{1,0:T(8,128)(2,1)S(1)}, bf16[720,128]{1,0:T(8,128)(2,1)S(1)}, u32[]{:S(2)}, u32[]{:S(2)}) %collective-permute-start.2) | collective-permute-done | bytes 184352 | tf_op jit(solution)/shard_map/ppermute | solution.py:354
  46.9 3.2 %collective-permute-done.1.rest_1_ = bf16[720,128]{1,0:T(8,128)(2,1)S(1)} collective-permute-done((bf16[720,128]{1,0:T(8,128)(2,1)S(1)}, bf16[720,128]{1,0:T(8,128)(2,1)S(1)}, u32[]{:S(2)}, u32[]{:S(2)}) %collective-permute-start.1) | collective-permute-done | bytes 184352 | tf_op jit(solution)/shard_map/ppermute | solution.py:354
  50.1 0.0 all-to-all-done.1.msg_ref
  50.1 0.0 copy-done.1
  50.1 0.0 copy-done
  50.1 1.2 %combine.1 = bf16[32,4,384]{2,1,0:T(4,128)(2,1)S(1)} custom-call(s32[3]{0:T(128)S(1)} %pad_add_fusion.info_ref, bf16[32,24,128]{2,1,0:T(8,128)(2,1)S(1)} %all-to-all-done.1.msg_ref, bf16[16,128]{1,0:T(8,128)(2,1)S(1)} %bitcast.10, bf16[16,1024]{1,0:T(8,128)(2,1)S(1)} %bitcast.8, bf16[720,128]{1,0:T(8,128)(2,1)S(1)} %pad_maximum_fusion.rest_0_, ...), custom_call_target="tpu_custom_call" | custom-call | tf_op jit(solution)/shard_map/combine/pallas_call | solution.py:305
  51.4 20.2 %all_to_all.20.in_ref = bf16[32,4,384]{2,1,0:T(4,128)(2,1)S(1)} all-to-all(bf16[32,4,384]{2,1,0:T(4,128)(2,1)S(1)} %combine.1), channel_id=1, replica_groups=mesh['grp'=8,'tp'=32] {'tp'}, dimensions={0} | all-to-all | bytes 196608 | tf_op jit(solution)/shard_map/all_to_all | solution.py:341
  71.6 14.2 %all_to_all.21.in_ref = bf16[32,4,384]{2,1,0:T(4,128)(2,1)S(1)} all-to-all(bf16[32,4,384]{2,1,0:T(4,128)(2,1)S(1)} %total.1), channel_id=1, replica_groups=mesh['grp'=8,'tp'=32] {'tp'}, dimensions={0} | all-to-all | bytes 196608 | tf_op jit(solution)/shard_map/all_to_all | solution.py:341
  85.8 0.8 finish.1
  (1 shorter events, 0.0 us)
Async XLA Ops:
  0.0 50.1 %copy-start.1 = (bf16[1,16,128]{2,1,0:T(8,128)(2,1)S(1)}, bf16[1,16,128]{2,1,0:T(8,128)(2,1)}, u32[]{:S(2)}) copy-start(bf16[1,16,128]{2,1,0:T(8,128)(2,1)} %param.10) | copy-start | bytes 12292
  0.0 50.1 %copy-start = (bf16[1,16,1024]{2,1,0:T(8,128)(2,1)S(1)}, bf16[1,16,1024]{2,1,0:T(8,128)(2,1)}, u32[]{:S(2)}) copy-start(bf16[1,16,1024]{2,1,0:T(8,128)(2,1)} %param.12) | copy-start | bytes 98308
  1.4 23.1 %all-to-all-start = ((bf16[32,16,128]{2,1,0:T(8,128)(2,1)}), bf16[32,16,128]{2,1,0:T(8,128)(2,1)S(1)}, u32[]{:S(2)}, u32[]{:S(2)}) async-start(bf16[32,16,128]{2,1,0:T(8,128)(2,1)} %copies.1), calls=%async_computation | async-start | bytes 262144 | tf_op jit(solution)/shard_map/all_to_all | solution.py:341
  14.0 4.8 %collective-permute-start = (bf16[360,128]{1,0:T(8,128)(2,1)}, bf16[360,128]{1,0:T(8,128)(2,1)S(1)}, u32[]{:S(2)}, u32[]{:S(2)}) collective-permute-start(bf16[360,128]{1,0:T(8,128)(2,1)} %bitcast.12), channel_id=1, source_target_pairs={{0,128},{32,160},{64,192},{96,224},{128,0},{160,32},{192,64},{224,... | collective-permute-start | bytes 276488 | tf_op jit(solution)/shard_map/ppermute | solution.py:354
  28.8 21.3 %all-to-all-start.1 = ((bf16[32,24,128]{2,1,0:T(8,128)(2,1)}), bf16[32,24,128]{2,1,0:T(8,128)(2,1)S(1)}, u32[]{:S(2)}, u32[]{:S(2)}) async-start(bf16[32,24,128]{2,1,0:T(8,128)(2,1)} %attend.1), calls=%async_computation.1 | async-start | bytes 393216 | tf_op jit(solution)/shard_map/all_to_all | solution.py:341
  34.9 8.2 %collective-permute-start.3 = (bf16[720,128]{1,0:T(8,128)(2,1)S(1)}, bf16[720,128]{1,0:T(8,128)(2,1)S(1)}, u32[]{:S(2)}, u32[]{:S(2)}) collective-permute-start(bf16[720,128]{1,0:T(8,128)(2,1)S(1)} %pad_maximum_fusion.rest_0_), channel_id=1, source_target_pairs={{0,96},{32,64},{64,32},{96,0},{128,224},{160,192},{192,160},{224,1... | collective-permute-start | bytes 552968 | tf_op jit(solution)/shard_map/ppermute | solution.py:354
  38.3 8.5 %collective-permute-start.2 = (bf16[720,128]{1,0:T(8,128)(2,1)S(1)}, bf16[720,128]{1,0:T(8,128)(2,1)S(1)}, u32[]{:S(2)}, u32[]{:S(2)}) collective-permute-start(bf16[720,128]{1,0:T(8,128)(2,1)S(1)} %pad_maximum_fusion.rest_0_), channel_id=1, source_target_pairs={{0,64},{32,96},{64,0},{96,32},{128,192},{160,224},{192,128},{224,1... | collective-permute-start | bytes 552968 | tf_op jit(solution)/shard_map/ppermute | solution.py:354
  42.0 8.1 %collective-permute-start.1 = (bf16[720,128]{1,0:T(8,128)(2,1)S(1)}, bf16[720,128]{1,0:T(8,128)(2,1)S(1)}, u32[]{:S(2)}, u32[]{:S(2)}) collective-permute-start(bf16[720,128]{1,0:T(8,128)(2,1)S(1)} %pad_maximum_fusion.rest_0_), channel_id=1, source_target_pairs={{0,32},{32,0},{64,96},{96,64},{128,160},{160,128},{192,224},{224,1... | collective-permute-start | bytes 552968 | tf_op jit(solution)/shard_map/ppermute | solution.py:354
where the time goes:
time: 87.9 us; the launch traced here: 86.6 us
  blocking collectives  34.4 us (39%)
  starting transfers between devices  26.2 us (30%)
  waiting for transfers between devices  16.5 us (19%)
  Pallas kernels  7.76 us (9%)
  other arithmetic  0.98 us (1%)
    all_to_all x2, blocking collectives, exchange(): return lax.all_to_all(pieces, axis, split_axis=0, concat_axis=0, tiled=True)  34.4 us
    all_to_all x2, starting transfers between devices, exchange(): return lax.all_to_all(pieces, axis, split_axis=0, concat_axis=0, tiled=True)  18.7 us
    ppermute x4, waiting for transfers between devices, from_pair(): return lax.ppermute(blocks, 'grp', [(i, i ^ step) for i in range(n_grp)])  11.7 us
    ppermute x4, starting transfers between devices, from_pair(): return lax.ppermute(blocks, 'grp', [(i, i ^ step) for i in range(n_grp)])  7.56 us
    all_to_all x2, waiting for transfers between devices, exchange(): return lax.all_to_all(pieces, axis, split_axis=0, concat_axis=0, tiled=True)  4.83 us
    pallas_call x1, Pallas kernels, attend(): pl.pallas_call(attend_kernel, out_shape=near_out((n_tp, MSG_ROWS, LANES),...  4.26 us
  transfers between devices with their start and end apart: 6, of which 5 were waited for; matrix products, arithmetic and copies ran while one was open for 1% of the time, Pallas kernels for 0%

commit v1 on v0

--- a/solution.py
+++ b/solution.py
@@ -18,9 +18,14 @@
 STAT_ROW = 16
 MSG_ROWS = 24
 INTERPRET = False
-STEPS = (4, 1, 2, 3)
+EARLY = (6, 7, 5, 2)
+LATE = (1, 3, 4)
 UNROLL = 2
-AHEAD = 2
+CHUNK = 4
+
+
+def axis_index(name):
+    return INTERPRET[name] if INTERPRET else lax.axis_index(name)
 
 
 def lane_iota(rows):
@@ -38,35 +43,54 @@
 
 
 def attend_kernel(
-    info_ref, lens_ref, table_ref, q_ref, pool_ref, out_ref, kv_scr, q_scr, num_scr, stat_scr, sems
+    size_ref, lens_ref, table_ref, q_ref, pool_ref, out_ref, kv_scr, q_scr, num_scr, stat_scr, sems
 ):
     n_tp, slots, _ = q_ref.shape
     pages = table_ref.shape[1]
     page_len = pool_ref.shape[1]
     kv_cols = KV_HEADS * HD
     tokens = pages * page_len
-    live_count = info_ref[0]
-    tp_index = info_ref[1]
+    live_count = size_ref[0]
+    tp_index = axis_index("tp")
     steps = (live_count + UNROLL - 1) // UNROLL
 
+    def live_length(slot):
+        return jnp.where(slot < live_count, lens_ref[slot], 0)
+
+    def is_live(slot, chunk):
+        first_page = chunk * CHUNK
+        return (first_page * n_tp + tp_index) * page_len < live_length(slot)
+
     def load_pages(slot):
-        for i in range(pages):
-            pltpu.make_async_copy(
-                pool_ref.at[table_ref[slot, i]], kv_scr.at[slot, i], sems.at[slot]
-            ).start()
+        for chunk in range(pages // CHUNK):
+
+            @pl.when(is_live(slot, chunk))
+            def _():
+                for i in range(chunk * CHUNK, (chunk + 1) * CHUNK):
+                    pltpu.make_async_copy(
+                        pool_ref.at[table_ref[slot, i]],
+                        kv_scr.at[slot, i],
+                        sems.at[slot, chunk],
+                    ).start()
+
+            @pl.when(jnp.logical_not(is_live(slot, chunk)))
+            def _():
+                kv_scr[slot, chunk * CHUNK : (chunk + 1) * CHUNK, :, kv_cols:] = jnp.zeros(
+                    (CHUNK, page_len, kv_cols), BF
+                )
 
     def wait_pages(slot):
-        pltpu.make_async_copy(
-            pool_ref.at[pl.ds(0, pages)], kv_scr.at[slot], sems.at[slot]
-        ).wait()
-
-    for step in range(AHEAD):
-
-        @pl.when(step < steps)
-        def _():
-            for i in range(UNROLL):
-                load_pages(step * UNROLL + i)
-
+        for chunk in range(pages // CHUNK):
+
+            @pl.when(is_live(slot, chunk))
+            def _():
+                pltpu.make_async_copy(
+                    pool_ref.at[pl.ds(0, CHUNK)],
+                    kv_scr.at[slot, pl.ds(chunk * CHUNK, CHUNK)],
+                    sems.at[slot, chunk],
+                ).wait()
+
+    lax.fori_loop(0, steps * UNROLL, lambda slot, _: load_pages(slot), None)
     q_scr[...] = (q_ref[...].astype(F32) * HD**-0.5).reshape(n_tp * slots, LANES)
     num_scr[...] = jnp.zeros_like(num_scr)
     low_half = lane_iota(n_tp) < HD
@@ -93,7 +117,7 @@
         )
 
     def slot_weights(slot, scores):
-        live = position < jnp.where(slot < live_count, lens_ref[slot], 0)
+        live = position < live_length(slot)
         scores = jnp.where(live, scores, NEG_BIG)
         top = jnp.max(scores, axis=1, keepdims=True)
         top = (top + jnp.abs(top) * 2.0**-7).astype(BF).astype(F32)
@@ -115,12 +139,6 @@
     def some_slots(step, state):
         tops, sums = state
         group = [step * UNROLL + i for i in range(UNROLL)]
-
-        @pl.when(step + AHEAD < steps)
-        def _():
-            for slot in group:
-                load_pages(slot + AHEAD * UNROLL)
-
         for slot in group:
             wait_pages(slot)
         scores = [slot_scores(slot) for slot in group]
@@ -147,15 +165,15 @@
         ).astype(BF)
 
 
-def combine_kernel(info_ref, msg_ref, q_ref, new_ref, *rest):
-    pair_refs, out_ref = rest[:-1], rest[-1]
+def combine_kernel(offsets, size_ref, msg_ref, q_ref, new_ref, *rest):
+    block_refs, out_ref = rest[:-1], rest[-1]
     n_tp = msg_ref.shape[0]
     slots = q_ref.shape[0]
-    live_count = info_ref[0]
-    tp_index = info_ref[1]
-    grp_index = info_ref[2]
-    blocks = 2 * len(pair_refs)
-    width = pair_refs[0].shape[0] // 2
+    live_count = size_ref[0]
+    tp_index = axis_index("tp")
+    grp_index = axis_index("grp")
+    blocks = len(block_refs)
+    width = block_refs[0].shape[0]
     ones_block = (
         lax.broadcasted_iota(jnp.int32, (LANES, LANES), 0) // HD
         == lax.broadcasted_iota(jnp.int32, (LANES, LANES), 1) // HD
@@ -211,15 +229,10 @@
     attended = jnp.where(slot < live_count, attended, 0.0).astype(BF)
     parts = n_tp // blocks
     rows = slots // parts
-    for k in range(blocks):
-        first = k % 2 * width
+    for offset, block_ref in zip(offsets, block_refs):
         share = lax.dot_general(
-            attended,
-            pair_refs[k // 2][first : first + width, :],
-            (((1,), (1,)), ((), ())),
-            preferred_element_type=F32,
+            attended, block_ref[...], (((1,), (1,)), ((), ())), preferred_element_type=F32
         ).astype(BF)
-        offset = (0, STEPS[0])[k % 2] ^ (0, *STEPS[1:])[k // 2]
         block = jnp.bitwise_xor(grp_index, offset)
         for i in range(parts):
             out_ref[block * parts + i, :, 0:width] = share[i * rows : (i + 1) * rows]
@@ -271,13 +284,13 @@
         out_shape=near_out((count, *piece.shape), piece.dtype),
         in_specs=[VMEM()],
         out_specs=VMEM(),
-        interpret=INTERPRET,
+        interpret=bool(INTERPRET),
         compiler_params=PARAMS,
         name="copies",
     )(far(piece))
 
 
-def attend(info, lens, table, gathered, pool):
+def attend(sizes, lens, table, gathered, pool):
     n_tp, slots, _ = gathered.shape
     return pl.pallas_call(
         attend_kernel,
@@ -289,28 +302,28 @@
             pltpu.VMEM((n_tp * slots, LANES), F32),
             pltpu.VMEM((slots * n_tp, LANES), F32),
             pltpu.VMEM((n_tp, LANES), F32),
-            pltpu.SemaphoreType.DMA((slots,)),
+            pltpu.SemaphoreType.DMA((slots, table.shape[1] // CHUNK)),
         ],
-        interpret=INTERPRET,
+        interpret=bool(INTERPRET),
         compiler_params=PARAMS,
         name="attend",
-    )(info, far(lens), far(table), near(gathered), far(pool))
-
-
-def combine(info, message, own, fresh, pairs):
+    )(sizes, far(lens), far(table), near(gathered), far(pool))
+
+
+def combine(sizes, message, own, fresh, blocks):
     n_tp = message.shape[0]
     slots = own.shape[0]
-    rows = slots * 2 * len(pairs) // n_tp
-    width = -(-pairs[0].shape[0] // 2 // LANES) * LANES
-    return pl.pallas_call(
-        combine_kernel,
+    rows = slots * len(blocks) // n_tp
+    width = -(-blocks[0].shape[0] // LANES) * LANES
+    return pl.pallas_call(
+        functools.partial(combine_kernel, tuple(blocks)),
         out_shape=near_out((n_tp, rows, width), BF),
-        in_specs=[SMEM()] + [VMEM()] * (3 + len(pairs)),
-        out_specs=VMEM(),
-        interpret=INTERPRET,
+        in_specs=[SMEM()] + [VMEM()] * (3 + len(blocks)),
+        out_specs=VMEM(),
+        interpret=bool(INTERPRET),
         compiler_params=PARAMS,
         name="combine",
-    )(info, near(message), near(own), near(fresh), *map(near, pairs))
+    )(sizes, near(message), near(own), near(fresh), *map(near, blocks.values()))
 
 
 def total_copies(pieces):
@@ -319,7 +332,7 @@
         out_shape=near_out(pieces.shape, BF),
         in_specs=[VMEM()],
         out_specs=VMEM(),
-        interpret=INTERPRET,
+        interpret=bool(INTERPRET),
         compiler_params=PARAMS,
         name="total",
     )(near(pieces))
@@ -331,7 +344,7 @@
         out_shape=jax.ShapeDtypeStruct((1, slots, width), F32),
         in_specs=[VMEM()],
         out_specs=VMEM(),
-        interpret=INTERPRET,
+        interpret=bool(INTERPRET),
         compiler_params=PARAMS,
         name="finish",
     )(near(pieces))
@@ -344,23 +357,23 @@
 def local(batch_sizes, seq_lens, page_table, queries, kv_pool, new_kv, out_weight):
     n_tp = lax.axis_size("tp")
     n_grp = lax.axis_size("grp")
-    tp_index = lax.axis_index("tp")
-    grp_index = lax.axis_index("grp")
     own = queries[0]
     slots = own.shape[0]
-    info = jnp.stack([batch_sizes[0], tp_index.astype(jnp.int32), grp_index.astype(jnp.int32)])
-
-    def from_pair(blocks, step):
-        return lax.ppermute(blocks, "grp", [(i, i ^ step) for i in range(n_grp)])
+
+    def from_pair(block, step):
+        return lax.ppermute(block, "grp", [(i, i ^ step) for i in range(n_grp)])
 
     own_block = out_weight.T
-    pair = jnp.concatenate([own_block, from_pair(own_block, STEPS[0])])
+    blocks = {0: own_block}
+    for step in EARLY:
+        blocks[step] = from_pair(own_block, step)
     gathered = exchange(copies(own, n_tp), "tp")
-    pair, gathered = lax.optimization_barrier((pair, gathered))
-    pairs = [pair] + [from_pair(pair, step) for step in STEPS[1:]]
-    message = attend(info, seq_lens[0], page_table[0], gathered, kv_pool[0])
+    message = attend(batch_sizes, seq_lens[0], page_table[0], gathered, kv_pool[0])
+    late_block, message = lax.optimization_barrier((own_block, message))
+    for step in LATE:
+        blocks[step] = from_pair(late_block, step)
     received = exchange(message, "tp")
-    shares = combine(info, received, own, new_kv[0], pairs)
+    shares = combine(batch_sizes, received, own, new_kv[0], blocks)
     totals = total_copies(exchange(shares, "tp"))
     return finish(exchange(totals, "tp"), slots, n_grp * out_weight.shape[1])
 

time: 87.9 us -> 90 us (1.024)
  starting transfers between devices: 26.2 us -> 30.9 us
  waiting for transfers between devices: 16.5 us -> 15.2 us
  other arithmetic: 0.98 us -> 0 us
    ppermute x4 -> x7, waiting for transfers between devices: 11.7 us -> 5.39 us  [from_pair(): return lax.ppermute(block, 'grp', [(i, i ^ step) for i in range(n_grp)])]
    ppermute x4 -> x7, starting transfers between devices: 7.56 us -> 13.2 us  [from_pair(): return lax.ppermute(block, 'grp', [(i, i ^ step) for i in range(n_grp)])]
    all_to_all x2, waiting for transfers between devices: 4.83 us -> 9.85 us  [exchange(): return lax.all_to_all(pieces, axis, split_axis=0, concat_axis=0, tiled=True)]
    concatenate x1 -> x0, other arithmetic: 0.9 us -> none  [local(): pair = jnp.concatenate([own_block, from_pair(own_block, STEPS[0])])]
  transfers between devices with their start and end apart: 6 -> 9, of which waited for: 5 -> 6; matrix products, arithmetic and copies ran while one was open for 1% -> 0% of each run, Pallas kernels for 0% -> 0%
where the time goes in v1:
time: 90 us; the launch traced here: 89.5 us
  blocking collectives  35.1 us (39%)
  starting transfers between devices  30.9 us (34%)
  waiting for transfers between devices  15.2 us (17%)
  Pallas kernels  7.53 us (8%)
    all_to_all x2, blocking collectives, exchange(): return lax.all_to_all(pieces, axis, split_axis=0, concat_axis=0, tiled=True)  35.1 us
    all_to_all x2, starting transfers between devices, exchange(): return lax.all_to_all(pieces, axis, split_axis=0, concat_axis=0, tiled=True)  17.8 us
    ppermute x7, starting transfers between devices, from_pair(): return lax.ppermute(block, 'grp', [(i, i ^ step) for i in range(n_grp)])  13.2 us
    all_to_all x2, waiting for transfers between devices, exchange(): return lax.all_to_all(pieces, axis, split_axis=0, concat_axis=0, tiled=True)  9.85 us
    ppermute x7, waiting for transfers between devices, from_pair(): return lax.ppermute(block, 'grp', [(i, i ^ step) for i in range(n_grp)])  5.39 us
    pallas_call x1, Pallas kernels, attend(): pl.pallas_call(attend_kernel, out_shape=near_out((n_tp, MSG_ROWS, LANES),...  4.57 us
  transfers between devices with their start and end apart: 9, of which 6 were waited for; matrix products, arithmetic and copies ran while one was open for 0% of the time, Pallas kernels for 0%

profile of v1, /device:TPU:1, one launch (start us, length us, event | category | flops | bytes accessed | tf_op | source)
XLA Modules:
  0.0 89.5 jit_solution(4685486625971552848)
XLA Ops:
  0.0 1.4 %copies.1 = bf16[32,16,128]{2,1,0:T(8,128)(2,1)} custom-call(bf16[16,128]{1,0:T(8,128)(2,1)} %bitcast.15), custom_call_target="tpu_custom_call" | custom-call | tf_op jit(solution)/shard_map/copies/pallas_call | solution.py:282
  1.4 12.6 %all-to-all-start = ((bf16[32,16,128]{2,1,0:T(8,128)(2,1)}), bf16[32,16,128]{2,1,0:T(8,128)(2,1)S(1)}, u32[]{:S(2)}, u32[]{:S(2)}) async-start(bf16[32,16,128]{2,1,0:T(8,128)(2,1)} %copies.1), calls=%async_computation | async-start | bytes 262144 | tf_op jit(solution)/shard_map/all_to_all | solution.py:354
  14.7 9.9 %all-to-all-done.q_ref = bf16[32,16,128]{2,1,0:T(8,128)(2,1)S(1)} async-done(((bf16[32,16,128]{2,1,0:T(8,128)(2,1)}), bf16[32,16,128]{2,1,0:T(8,128)(2,1)S(1)}, u32[]{:S(2)}, u32[]{:S(2)}) %all-to-all-start) | async-done | bytes 131104 | tf_op jit(solution)/shard_map/all_to_all | solution.py:354
  24.5 4.6 %attend.1 = bf16[32,24,128]{2,1,0:T(8,128)(2,1)} custom-call(s32[1]{0:T(128)S(6)} %copy.8.size_ref, s32[16]{0:T(128)} %bitcast.19, s32[16,16]{1,0:T(8,128)} %bitcast.18, bf16[32,16,128]{2,1,0:T(8,128)(2,1)S(1)} %all-to-all-done.q_ref, bf16[256,16,1024]{2,1,0:T(8,128)(2,1)} %bitcast.17), custom_call_target="tpu_custom_call" | custom-call | tf_op jit(solution)/shard_map/attend/pallas_call | solution.py:295
  29.1 5.2 %all-to-all-start.1 = ((bf16[32,24,128]{2,1,0:T(8,128)(2,1)}), bf16[32,24,128]{2,1,0:T(8,128)(2,1)S(1)}, u32[]{:S(2)}, u32[]{:S(2)}) async-start(bf16[32,24,128]{2,1,0:T(8,128)(2,1)} %attend.1), calls=%async_computation.1 | async-start | bytes 393216 | tf_op jit(solution)/shard_map/all_to_all | solution.py:354
  34.3 7.3 %collective-permute-start.3 = (bf16[360,128]{1,0:T(8,128)(2,1)S(1)}, bf16[360,128]{1,0:T(8,128)(2,1)S(1)}, u32[]{:S(2)}, u32[]{:S(2)}) collective-permute-start(bf16[360,128]{1,0:T(8,128)(2,1)S(1)} %bitcast.6), channel_id=1, source_target_pairs={{0,64},{32,96},{64,0},{96,32},{128,192},{160,224},{192,128},{224,1... | collective-permute-start | bytes 276488 | tf_op jit(solution)/shard_map/ppermute | solution.py:364
  41.6 0.0 collective-permute-start.2
  41.6 1.3 %collective-permute-start.1 = (bf16[360,128]{1,0:T(8,128)(2,1)S(1)}, bf16[360,128]{1,0:T(8,128)(2,1)S(1)}, u32[]{:S(2)}, u32[]{:S(2)}) collective-permute-start(bf16[360,128]{1,0:T(8,128)(2,1)S(1)} %bitcast.8), channel_id=1, source_target_pairs={{0,224},{32,192},{64,160},{96,128},{128,96},{160,64},{192,32},{224... | collective-permute-start | bytes 276488 | tf_op jit(solution)/shard_map/ppermute | solution.py:364
  42.9 1.3 %collective-permute-start = (bf16[360,128]{1,0:T(8,128)(2,1)S(1)}, bf16[360,128]{1,0:T(8,128)(2,1)S(1)}, u32[]{:S(2)}, u32[]{:S(2)}) collective-permute-start(bf16[360,128]{1,0:T(8,128)(2,1)S(1)} %bitcast.9), channel_id=1, source_target_pairs={{0,192},{32,224},{64,128},{96,160},{128,64},{160,96},{192,0},{224,... | collective-permute-start | bytes 276488 | tf_op jit(solution)/shard_map/ppermute | solution.py:364
  44.2 2.8 %collective-permute-start.6 = (bf16[360,128]{1,0:T(8,128)(2,1)S(1)}, bf16[360,128]{1,0:T(8,128)(2,1)S(1)}, u32[]{:S(2)}, u32[]{:S(2)}) collective-permute-start(bf16[360,128]{1,0:T(8,128)(2,1)S(1)} %bitcast.10), channel_id=1, source_target_pairs={{0,128},{32,160},{64,192},{96,224},{128,0},{160,32},{192,64},{224,... | collective-permute-start | bytes 276488 | tf_op jit(solution)/shard_map/ppermute | solution.py:364
  47.0 0.0 collective-permute-done.3.rest_4_
  47.0 0.0 collective-permute-start.5
  47.0 0.3 collective-permute-done.2.rest_3_
  47.3 0.5 collective-permute-start.4
  47.8 0.0 collective-permute-done.1.rest_2_
  47.8 1.6 %collective-permute-done.rest_1_ = bf16[360,128]{1,0:T(8,128)(2,1)S(1)} collective-permute-done((bf16[360,128]{1,0:T(8,128)(2,1)S(1)}, bf16[360,128]{1,0:T(8,128)(2,1)S(1)}, u32[]{:S(2)}, u32[]{:S(2)}) %collective-permute-start) | collective-permute-done | bytes 92192 | tf_op jit(solution)/shard_map/ppermute | solution.py:364
  49.4 1.1 %collective-permute-done.6.rest_7_ = bf16[360,128]{1,0:T(8,128)(2,1)S(1)} collective-permute-done((bf16[360,128]{1,0:T(8,128)(2,1)S(1)}, bf16[360,128]{1,0:T(8,128)(2,1)S(1)}, u32[]{:S(2)}, u32[]{:S(2)}) %collective-permute-start.6) | collective-permute-done | bytes 92192 | tf_op jit(solution)/shard_map/ppermute | solution.py:364
  50.5 1.3 %collective-permute-done.5.rest_6_ = bf16[360,128]{1,0:T(8,128)(2,1)S(1)} collective-permute-done((bf16[360,128]{1,0:T(8,128)(2,1)S(1)}, bf16[360,128]{1,0:T(8,128)(2,1)S(1)}, u32[]{:S(2)}, u32[]{:S(2)}) %collective-permute-start.5) | collective-permute-done | bytes 92192 | tf_op jit(solution)/shard_map/ppermute | solution.py:364
  51.9 1.0 %collective-permute-done.4.rest_5_ = bf16[360,128]{1,0:T(8,128)(2,1)S(1)} collective-permute-done((bf16[360,128]{1,0:T(8,128)(2,1)S(1)}, bf16[360,128]{1,0:T(8,128)(2,1)S(1)}, u32[]{:S(2)}, u32[]{:S(2)}) %collective-permute-start.4) | collective-permute-done | bytes 92192 | tf_op jit(solution)/shard_map/ppermute | solution.py:364
  52.9 0.0 all-to-all-done.1.msg_ref
  52.9 0.7 combine.1
  53.6 20.9 %all_to_all.20.in_ref = bf16[32,4,384]{2,1,0:T(4,128)(2,1)S(1)} all-to-all(bf16[32,4,384]{2,1,0:T(4,128)(2,1)S(1)} %combine.1), channel_id=1, replica_groups=mesh['grp'=8,'tp'=32] {'tp'}, dimensions={0} | all-to-all | bytes 196608 | tf_op jit(solution)/shard_map/all_to_all | solution.py:354
  74.5 14.2 %all_to_all.21.in_ref = bf16[32,4,384]{2,1,0:T(4,128)(2,1)S(1)} all-to-all(bf16[32,4,384]{2,1,0:T(4,128)(2,1)S(1)} %total.1), channel_id=1, replica_groups=mesh['grp'=8,'tp'=32] {'tp'}, dimensions={0} | all-to-all | bytes 196608 | tf_op jit(solution)/shard_map/all_to_all | solution.py:354
  88.7 0.8 finish.1
  (7 shorter events, 0.1 us)
Async XLA Ops:
  0.0 52.9 %copy-start.2 = (bf16[1,16,128]{2,1,0:T(8,128)(2,1)S(1)}, bf16[1,16,128]{2,1,0:T(8,128)(2,1)}, u32[]{:S(2)}) copy-start(bf16[1,16,128]{2,1,0:T(8,128)(2,1)} %param.10) | copy-start | bytes 12292
  0.0 34.3 %copy-start = (bf16[128,360]{0,1:T(8,128)(2,1)S(1)}, bf16[128,360]{0,1:T(8,128)(2,1)}, u32[]{:S(2)}) copy-start(bf16[128,360]{0,1:T(8,128)(2,1)} %param.13) | copy-start | bytes 276484
  0.0 52.9 %copy-start.1 = (bf16[1,16,1024]{2,1,0:T(8,128)(2,1)S(1)}, bf16[1,16,1024]{2,1,0:T(8,128)(2,1)}, u32[]{:S(2)}) copy-start(bf16[1,16,1024]{2,1,0:T(8,128)(2,1)} %param.12) | copy-start | bytes 98308
  1.4 23.1 %all-to-all-start = ((bf16[32,16,128]{2,1,0:T(8,128)(2,1)}), bf16[32,16,128]{2,1,0:T(8,128)(2,1)S(1)}, u32[]{:S(2)}, u32[]{:S(2)}) async-start(bf16[32,16,128]{2,1,0:T(8,128)(2,1)} %copies.1), calls=%async_computation | async-start | bytes 262144 | tf_op jit(solution)/shard_map/all_to_all | solution.py:354
  29.1 23.8 %all-to-all-start.1 = ((bf16[32,24,128]{2,1,0:T(8,128)(2,1)}), bf16[32,24,128]{2,1,0:T(8,128)(2,1)S(1)}, u32[]{:S(2)}, u32[]{:S(2)}) async-start(bf16[32,24,128]{2,1,0:T(8,128)(2,1)} %attend.1), calls=%async_computation.1 | async-start | bytes 393216 | tf_op jit(solution)/shard_map/all_to_all | solution.py:354
  34.3 12.7 %collective-permute-start.3 = (bf16[360,128]{1,0:T(8,128)(2,1)S(1)}, bf16[360,128]{1,0:T(8,128)(2,1)S(1)}, u32[]{:S(2)}, u32[]{:S(2)}) collective-permute-start(bf16[360,128]{1,0:T(8,128)(2,1)S(1)} %bitcast.6), channel_id=1, source_target_pairs={{0,64},{32,96},{64,0},{96,32},{128,192},{160,224},{192,128},{224,1... | collective-permute-start | bytes 276488 | tf_op jit(solution)/shard_map/ppermute | solution.py:364
  41.6 5.7 %collective-permute-start.2 = (bf16[360,128]{1,0:T(8,128)(2,1)S(1)}, bf16[360,128]{1,0:T(8,128)(2,1)S(1)}, u32[]{:S(2)}, u32[]{:S(2)}) collective-permute-start(bf16[360,128]{1,0:T(8,128)(2,1)S(1)} %bitcast.7), channel_id=1, source_target_pairs={{0,160},{32,128},{64,224},{96,192},{128,32},{160,0},{192,96},{224,... | collective-permute-start | bytes 276488 | tf_op jit(solution)/shard_map/ppermute | solution.py:364
  41.6 6.2 %collective-permute-start.1 = (bf16[360,128]{1,0:T(8,128)(2,1)S(1)}, bf16[360,128]{1,0:T(8,128)(2,1)S(1)}, u32[]{:S(2)}, u32[]{:S(2)}) collective-permute-start(bf16[360,128]{1,0:T(8,128)(2,1)S(1)} %bitcast.8), channel_id=1, source_target_pairs={{0,224},{32,192},{64,160},{96,128},{128,96},{160,64},{192,32},{224... | collective-permute-start | bytes 276488 | tf_op jit(solution)/shard_map/ppermute | solution.py:364
  42.9 6.5 %collective-permute-start = (bf16[360,128]{1,0:T(8,128)(2,1)S(1)}, bf16[360,128]{1,0:T(8,128)(2,1)S(1)}, u32[]{:S(2)}, u32[]{:S(2)}) collective-permute-start(bf16[360,128]{1,0:T(8,128)(2,1)S(1)} %bitcast.9), channel_id=1, source_target_pairs={{0,192},{32,224},{64,128},{96,160},{128,64},{160,96},{192,0},{224,... | collective-permute-start | bytes 276488 | tf_op jit(solution)/shard_map/ppermute | solution.py:364
  44.2 6.3 %collective-permute-start.6 = (bf16[360,128]{1,0:T(8,128)(2,1)S(1)}, bf16[360,128]{1,0:T(8,128)(2,1)S(1)}, u32[]{:S(2)}, u32[]{:S(2)}) collective-permute-start(bf16[360,128]{1,0:T(8,128)(2,1)S(1)} %bitcast.10), channel_id=1, source_target_pairs={{0,128},{32,160},{64,192},{96,224},{128,0},{160,32},{192,64},{224,... | collective-permute-start | bytes 276488 | tf_op jit(solution)/shard_map/ppermute | solution.py:364
  47.0 4.9 %collective-permute-start.5 = (bf16[360,128]{1,0:T(8,128)(2,1)S(1)}, bf16[360,128]{1,0:T(8,128)(2,1)S(1)}, u32[]{:S(2)}, u32[]{:S(2)}) collective-permute-start(bf16[360,128]{1,0:T(8,128)(2,1)S(1)} %bitcast.11), channel_id=1, source_target_pairs={{0,96},{32,64},{64,32},{96,0},{128,224},{160,192},{192,160},{224,1... | collective-permute-start | bytes 276488 | tf_op jit(solution)/shard_map/ppermute | solution.py:364
  47.3 5.5 %collective-permute-start.4 = (bf16[360,128]{1,0:T(8,128)(2,1)S(1)}, bf16[360,128]{1,0:T(8,128)(2,1)S(1)}, u32[]{:S(2)}, u32[]{:S(2)}) collective-permute-start(bf16[360,128]{1,0:T(8,128)(2,1)S(1)} %bitcast.12), channel_id=1, source_target_pairs={{0,32},{32,0},{64,96},{96,64},{128,160},{160,128},{192,224},{224,1... | collective-permute-start | bytes 276488 | tf_op jit(solution)/shard_map/ppermute | solution.py:364

commit v2 on v1

--- a/solution.py
+++ b/solution.py
@@ -18,8 +18,8 @@
 STAT_ROW = 16
 MSG_ROWS = 24
 INTERPRET = False
-EARLY = (6, 7, 5, 2)
-LATE = (1, 3, 4)
+FIRST_STEP = 4
+PAIR_STEPS = (2, 3, 1)
 UNROLL = 2
 CHUNK = 4
 
@@ -166,14 +166,14 @@
 
 
 def combine_kernel(offsets, size_ref, msg_ref, q_ref, new_ref, *rest):
-    block_refs, out_ref = rest[:-1], rest[-1]
+    pair_refs, out_ref = rest[:-1], rest[-1]
     n_tp = msg_ref.shape[0]
     slots = q_ref.shape[0]
     live_count = size_ref[0]
     tp_index = axis_index("tp")
     grp_index = axis_index("grp")
-    blocks = len(block_refs)
-    width = block_refs[0].shape[0]
+    blocks = 2 * len(pair_refs)
+    width = pair_refs[0].shape[0] // 2
     ones_block = (
         lax.broadcasted_iota(jnp.int32, (LANES, LANES), 0) // HD
         == lax.broadcasted_iota(jnp.int32, (LANES, LANES), 1) // HD
@@ -229,13 +229,17 @@
     attended = jnp.where(slot < live_count, attended, 0.0).astype(BF)
     parts = n_tp // blocks
     rows = slots // parts
-    for offset, block_ref in zip(offsets, block_refs):
-        share = lax.dot_general(
-            attended, block_ref[...], (((1,), (1,)), ((), ())), preferred_element_type=F32
-        ).astype(BF)
-        block = jnp.bitwise_xor(grp_index, offset)
-        for i in range(parts):
-            out_ref[block * parts + i, :, 0:width] = share[i * rows : (i + 1) * rows]
+    for offset, pair_ref in zip(offsets, pair_refs):
+        for half in range(2):
+            share = lax.dot_general(
+                attended,
+                pair_ref[half * width : (half + 1) * width, :],
+                (((1,), (1,)), ((), ())),
+                preferred_element_type=F32,
+            ).astype(BF)
+            block = jnp.bitwise_xor(grp_index, offset ^ (half * FIRST_STEP))
+            for i in range(parts):
+                out_ref[block * parts + i, :, 0:width] = share[i * rows : (i + 1) * rows]
 
 
 def copies_kernel(in_ref, out_ref):
@@ -310,20 +314,20 @@
     )(sizes, far(lens), far(table), near(gathered), far(pool))
 
 
-def combine(sizes, message, own, fresh, blocks):
+def combine(sizes, message, own, fresh, pairs):
     n_tp = message.shape[0]
     slots = own.shape[0]
-    rows = slots * len(blocks) // n_tp
-    width = -(-blocks[0].shape[0] // LANES) * LANES
-    return pl.pallas_call(
-        functools.partial(combine_kernel, tuple(blocks)),
+    rows = slots * 2 * len(pairs) // n_tp
+    width = -(-pairs[0].shape[0] // 2 // LANES) * LANES
+    return pl.pallas_call(
+        functools.partial(combine_kernel, tuple(pairs)),
         out_shape=near_out((n_tp, rows, width), BF),
-        in_specs=[SMEM()] + [VMEM()] * (3 + len(blocks)),
+        in_specs=[SMEM()] + [VMEM()] * (3 + len(pairs)),
         out_specs=VMEM(),
         interpret=bool(INTERPRET),
         compiler_params=PARAMS,
         name="combine",
-    )(sizes, near(message), near(own), near(fresh), *map(near, blocks.values()))
+    )(sizes, near(message), near(own), near(fresh), *map(near, pairs.values()))
 
 
 def total_copies(pieces):
@@ -364,16 +368,13 @@
         return lax.ppermute(block, "grp", [(i, i ^ step) for i in range(n_grp)])
 
     own_block = out_weight.T
-    blocks = {0: own_block}
-    for step in EARLY:
-        blocks[step] = from_pair(own_block, step)
-    gathered = exchange(copies(own, n_tp), "tp")
+    pair = jnp.concatenate([own_block, from_pair(own_block, FIRST_STEP)])
+    pairs = {0: pair, **{step: from_pair(pair, step) for step in PAIR_STEPS}}
+    fanned = copies(own, n_tp)
+    gathered = exchange(fanned, "tp")
     message = attend(batch_sizes, seq_lens[0], page_table[0], gathered, kv_pool[0])
-    late_block, message = lax.optimization_barrier((own_block, message))
-    for step in LATE:
-        blocks[step] = from_pair(late_block, step)
     received = exchange(message, "tp")
-    shares = combine(batch_sizes, received, own, new_kv[0], blocks)
+    shares = combine(batch_sizes, received, own, new_kv[0], pairs)
     totals = total_copies(exchange(shares, "tp"))
     return finish(exchange(totals, "tp"), slots, n_grp * out_weight.shape[1])
 

time: 90 us -> 87 us (0.967)
  starting transfers between devices: 30.9 us -> 25.8 us
  waiting for transfers between devices: 15.2 us -> 17.7 us
    ppermute x7 -> x4, starting transfers between devices: 13.2 us -> 8.01 us  [from_pair(): return lax.ppermute(block, 'grp', [(i, i ^ step) for i in range(n_grp)])]
    ppermute x7 -> x4, waiting for transfers between devices: 5.39 us -> 8.24 us  [from_pair(): return lax.ppermute(block, 'grp', [(i, i ^ step) for i in range(n_grp)])]
  transfers between devices with their start and end apart: 9 -> 6, of which waited for: 6 -> 3; matrix products, arithmetic and copies ran while one was open for 0% -> 0% of each run, Pallas kernels for 0% -> 5%
where the time goes in v2:
time: 87 us; the launch traced here: 86.5 us
  blocking collectives  34.7 us (40%)
  starting transfers between devices  25.8 us (30%)
  waiting for transfers between devices  17.7 us (20%)
  Pallas kernels  7.52 us (9%)
    all_to_all x2, blocking collectives, exchange(): return lax.all_to_all(pieces, axis, split_axis=0, concat_axis=0, tiled=True)  34.7 us
    all_to_all x2, starting transfers between devices, exchange(): return lax.all_to_all(pieces, axis, split_axis=0, concat_axis=0, tiled=True)  17.8 us
    all_to_all x2, waiting for transfers between devices, exchange(): return lax.all_to_all(pieces, axis, split_axis=0, concat_axis=0, tiled=True)  9.45 us
    ppermute x4, waiting for transfers between devices, from_pair(): return lax.ppermute(block, 'grp', [(i, i ^ step) for i in range(n_grp)])  8.24 us
    ppermute x4, starting transfers between devices, from_pair(): return lax.ppermute(block, 'grp', [(i, i ^ step) for i in range(n_grp)])  8.01 us
    pallas_call x1, Pallas kernels, attend(): pl.pallas_call(attend_kernel, out_shape=near_out((n_tp, MSG_ROWS, LANES),...  4.57 us
  transfers between devices with their start and end apart: 6, of which 3 were waited for; matrix products, arithmetic and copies ran while one was open for 0% of the time, Pallas kernels for 5%

profile of v2, /device:TPU:1, one launch (start us, length us, event | category | flops | bytes accessed | tf_op | source)
XLA Modules:
  0.0 86.5 jit_solution(633913145255514139)
XLA Ops:
  0.0 0.0 copy-start.1
  0.0 0.0 copy-start.2
  0.0 0.0 copy-start
  0.0 1.4 %copies.1 = bf16[32,16,128]{2,1,0:T(8,128)(2,1)} custom-call(bf16[16,128]{1,0:T(8,128)(2,1)} %bitcast.7), custom_call_target="tpu_custom_call" | custom-call | tf_op jit(solution)/shard_map/copies/pallas_call | solution.py:286
  1.4 12.6 %all-to-all-start = ((bf16[32,16,128]{2,1,0:T(8,128)(2,1)}), bf16[32,16,128]{2,1,0:T(8,128)(2,1)S(1)}, u32[]{:S(2)}, u32[]{:S(2)}) async-start(bf16[32,16,128]{2,1,0:T(8,128)(2,1)} %copies.1), calls=%async_computation | async-start | bytes 262144 | tf_op jit(solution)/shard_map/all_to_all | solution.py:358
  14.0 0.4 collective-permute-start
  15.1 9.4 %all-to-all-done.q_ref = bf16[32,16,128]{2,1,0:T(8,128)(2,1)S(1)} async-done(((bf16[32,16,128]{2,1,0:T(8,128)(2,1)}), bf16[32,16,128]{2,1,0:T(8,128)(2,1)S(1)}, u32[]{:S(2)}, u32[]{:S(2)}) %all-to-all-start) | async-done | bytes 131104 | tf_op jit(solution)/shard_map/all_to_all | solution.py:358
  24.5 4.6 %attend.1 = bf16[32,24,128]{2,1,0:T(8,128)(2,1)} custom-call(s32[1]{0:T(128)S(6)} %copy.8.size_ref, s32[16]{0:T(128)} %bitcast.13, s32[16,16]{1,0:T(8,128)} %bitcast.12, bf16[32,16,128]{2,1,0:T(8,128)(2,1)S(1)} %all-to-all-done.q_ref, bf16[256,16,1024]{2,1,0:T(8,128)(2,1)} %bitcast.9), custom_call_target="tpu_custom_call" | custom-call | tf_op jit(solution)/shard_map/attend/pallas_call | solution.py:299
  29.1 5.2 %all-to-all-start.1 = ((bf16[32,24,128]{2,1,0:T(8,128)(2,1)}), bf16[32,24,128]{2,1,0:T(8,128)(2,1)S(1)}, u32[]{:S(2)}, u32[]{:S(2)}) async-start(bf16[32,24,128]{2,1,0:T(8,128)(2,1)} %attend.1), calls=%async_computation.1 | async-start | bytes 393216 | tf_op jit(solution)/shard_map/all_to_all | solution.py:358
  34.3 0.0 collective-permute-done
  34.3 0.0 copy-done.2
  34.3 0.6 collective-permute-start.3
  34.9 7.0 %collective-permute-start.2 = (bf16[720,128]{1,0:T(8,128)(2,1)S(1)}, bf16[720,128]{1,0:T(8,128)(2,1)S(1)}, u32[]{:S(2)}, u32[]{:S(2)}) collective-permute-start(bf16[720,128]{1,0:T(8,128)(2,1)S(1)} %pad_maximum_fusion.rest_0_), channel_id=1, source_target_pairs={{0,96},{32,64},{64,32},{96,0},{128,224},{160,192},{192,160},{224,1... | collective-permute-start | bytes 552968 | tf_op jit(solution)/shard_map/ppermute | solution.py:368
  41.9 0.0 collective-permute-start.1
  41.9 0.0 collective-permute-done.3.rest_3_
  42.0 8.0 %collective-permute-done.2.rest_2_ = bf16[720,128]{1,0:T(8,128)(2,1)S(1)} collective-permute-done((bf16[720,128]{1,0:T(8,128)(2,1)S(1)}, bf16[720,128]{1,0:T(8,128)(2,1)S(1)}, u32[]{:S(2)}, u32[]{:S(2)}) %collective-permute-start.2) | collective-permute-done | bytes 184352 | tf_op jit(solution)/shard_map/ppermute | solution.py:368
  50.0 0.2 collective-permute-done.1.rest_1_
  50.2 0.0 all-to-all-done.1.msg_ref
  50.2 0.0 copy-done.1
  50.2 0.0 copy-done
  50.2 0.7 combine.1
  50.9 20.5 %all_to_all.20.in_ref = bf16[32,4,384]{2,1,0:T(4,128)(2,1)S(1)} all-to-all(bf16[32,4,384]{2,1,0:T(4,128)(2,1)S(1)} %combine.1), channel_id=1, replica_groups=mesh['grp'=8,'tp'=32] {'tp'}, dimensions={0} | all-to-all | bytes 196608 | tf_op jit(solution)/shard_map/all_to_all | solution.py:358
  71.5 14.2 %all_to_all.21.in_ref = bf16[32,4,384]{2,1,0:T(4,128)(2,1)S(1)} all-to-all(bf16[32,4,384]{2,1,0:T(4,128)(2,1)S(1)} %total.1), channel_id=1, replica_groups=mesh['grp'=8,'tp'=32] {'tp'}, dimensions={0} | all-to-all | bytes 196608 | tf_op jit(solution)/shard_map/all_to_all | solution.py:358
  85.7 0.8 finish.1
  (2 shorter events, 0.1 us)
Async XLA Ops:
  0.0 50.2 %copy-start.1 = (bf16[1,16,128]{2,1,0:T(8,128)(2,1)S(1)}, bf16[1,16,128]{2,1,0:T(8,128)(2,1)}, u32[]{:S(2)}) copy-start(bf16[1,16,128]{2,1,0:T(8,128)(2,1)} %param.10) | copy-start | bytes 12292
  0.0 34.3 %copy-start.2 = (bf16[128,360]{0,1:T(8,128)(2,1)S(1)}, bf16[128,360]{0,1:T(8,128)(2,1)}, u32[]{:S(2)}) copy-start(bf16[128,360]{0,1:T(8,128)(2,1)} %param.13) | copy-start | bytes 276484
  0.0 50.2 %copy-start = (bf16[1,16,1024]{2,1,0:T(8,128)(2,1)S(1)}, bf16[1,16,1024]{2,1,0:T(8,128)(2,1)}, u32[]{:S(2)}) copy-start(bf16[1,16,1024]{2,1,0:T(8,128)(2,1)} %param.12) | copy-start | bytes 98308
  1.4 23.1 %all-to-all-start = ((bf16[32,16,128]{2,1,0:T(8,128)(2,1)}), bf16[32,16,128]{2,1,0:T(8,128)(2,1)S(1)}, u32[]{:S(2)}, u32[]{:S(2)}) async-start(bf16[32,16,128]{2,1,0:T(8,128)(2,1)} %copies.1), calls=%async_computation | async-start | bytes 262144 | tf_op jit(solution)/shard_map/all_to_all | solution.py:358
  14.0 20.3 %collective-permute-start = (bf16[360,128]{1,0:T(8,128)(2,1)}, bf16[360,128]{1,0:T(8,128)(2,1)S(1)}, u32[]{:S(2)}, u32[]{:S(2)}) collective-permute-start(bf16[360,128]{1,0:T(8,128)(2,1)} %bitcast.10), channel_id=1, source_target_pairs={{0,128},{32,160},{64,192},{96,224},{128,0},{160,32},{192,64},{224,... | collective-permute-start | bytes 276488 | tf_op jit(solution)/shard_map/ppermute | solution.py:368
  29.1 21.1 %all-to-all-start.1 = ((bf16[32,24,128]{2,1,0:T(8,128)(2,1)}), bf16[32,24,128]{2,1,0:T(8,128)(2,1)S(1)}, u32[]{:S(2)}, u32[]{:S(2)}) async-start(bf16[32,24,128]{2,1,0:T(8,128)(2,1)} %attend.1), calls=%async_computation.1 | async-start | bytes 393216 | tf_op jit(solution)/shard_map/all_to_all | solution.py:358
  34.3 7.6 %collective-permute-start.3 = (bf16[720,128]{1,0:T(8,128)(2,1)S(1)}, bf16[720,128]{1,0:T(8,128)(2,1)S(1)}, u32[]{:S(2)}, u32[]{:S(2)}) collective-permute-start(bf16[720,128]{1,0:T(8,128)(2,1)S(1)} %pad_maximum_fusion.rest_0_), channel_id=1, source_target_pairs={{0,32},{32,0},{64,96},{96,64},{128,160},{160,128},{192,224},{224,1... | collective-permute-start | bytes 552968 | tf_op jit(solution)/shard_map/ppermute | solution.py:368
  34.9 15.0 %collective-permute-start.2 = (bf16[720,128]{1,0:T(8,128)(2,1)S(1)}, bf16[720,128]{1,0:T(8,128)(2,1)S(1)}, u32[]{:S(2)}, u32[]{:S(2)}) collective-permute-start(bf16[720,128]{1,0:T(8,128)(2,1)S(1)} %pad_maximum_fusion.rest_0_), channel_id=1, source_target_pairs={{0,96},{32,64},{64,32},{96,0},{128,224},{160,192},{192,160},{224,1... | collective-permute-start | bytes 552968 | tf_op jit(solution)/shard_map/ppermute | solution.py:368
  41.9 8.2 %collective-permute-start.1 = (bf16[720,128]{1,0:T(8,128)(2,1)S(1)}, bf16[720,128]{1,0:T(8,128)(2,1)S(1)}, u32[]{:S(2)}, u32[]{:S(2)}) collective-permute-start(bf16[720,128]{1,0:T(8,128)(2,1)S(1)} %pad_maximum_fusion.rest_0_), channel_id=1, source_target_pairs={{0,64},{32,96},{64,0},{96,32},{128,192},{160,224},{192,128},{224,1... | collective-permute-start | bytes 552968 | tf_op jit(solution)/shard_map/ppermute | solution.py:368

commit v3 on v2

--- a/solution.py
+++ b/solution.py
@@ -21,7 +21,6 @@
 FIRST_STEP = 4
 PAIR_STEPS = (2, 3, 1)
 UNROLL = 2
-CHUNK = 4
 
 
 def axis_index(name):
@@ -43,10 +42,10 @@
 
 
 def attend_kernel(
-    size_ref, lens_ref, table_ref, q_ref, pool_ref, out_ref, kv_scr, q_scr, num_scr, stat_scr, sems
+    size_ref, lens_ref, table_ref, q_ref, pool_ref, out_ref, num_scr, stat_scr
 ):
-    n_tp, slots, _ = q_ref.shape
-    pages = table_ref.shape[1]
+    slots, pages = table_ref.shape
+    n_tp = q_ref.shape[0] // slots
     page_len = pool_ref.shape[1]
     kv_cols = KV_HEADS * HD
     tokens = pages * page_len
@@ -57,41 +56,6 @@
     def live_length(slot):
         return jnp.where(slot < live_count, lens_ref[slot], 0)
 
-    def is_live(slot, chunk):
-        first_page = chunk * CHUNK
-        return (first_page * n_tp + tp_index) * page_len < live_length(slot)
-
-    def load_pages(slot):
-        for chunk in range(pages // CHUNK):
-
-            @pl.when(is_live(slot, chunk))
-            def _():
-                for i in range(chunk * CHUNK, (chunk + 1) * CHUNK):
-                    pltpu.make_async_copy(
-                        pool_ref.at[table_ref[slot, i]],
-                        kv_scr.at[slot, i],
-                        sems.at[slot, chunk],
-                    ).start()
-
-            @pl.when(jnp.logical_not(is_live(slot, chunk)))
-            def _():
-                kv_scr[slot, chunk * CHUNK : (chunk + 1) * CHUNK, :, kv_cols:] = jnp.zeros(
-                    (CHUNK, page_len, kv_cols), BF
-                )
-
-    def wait_pages(slot):
-        for chunk in range(pages // CHUNK):
-
-            @pl.when(is_live(slot, chunk))
-            def _():
-                pltpu.make_async_copy(
-                    pool_ref.at[pl.ds(0, CHUNK)],
-                    kv_scr.at[slot, pl.ds(chunk * CHUNK, CHUNK)],
-                    sems.at[slot, chunk],
-                ).wait()
-
-    lax.fori_loop(0, steps * UNROLL, lambda slot, _: load_pages(slot), None)
-    q_scr[...] = (q_ref[...].astype(F32) * HD**-0.5).reshape(n_tp * slots, LANES)
     num_scr[...] = jnp.zeros_like(num_scr)
     low_half = lane_iota(n_tp) < HD
     own_block = (
@@ -103,15 +67,15 @@
     lane = lane_iota(HEADS)
 
     def slot_queries(slot):
-        x = q_scr[pl.ds(slot, n_tp, stride=slots), :]
+        x = q_ref[pl.ds(slot, n_tp, stride=slots), :]
         turned = roll_lanes(x, HD)
         even = jnp.where(low_half, x, turned)
         odd = jnp.where(low_half, turned, x)
         wide = [jnp.where(own_block, jnp.concatenate([h] * 4, axis=1), 0.0) for h in (even, odd)]
         return jnp.concatenate(wide, axis=0).astype(BF)
 
-    def slot_scores(slot):
-        keys = kv_scr[slot, :, :, 0:kv_cols].reshape(tokens, kv_cols)
+    def slot_scores(slot, ids):
+        keys = jnp.concatenate([pool_ref[i, :, 0:kv_cols] for i in ids], axis=0)
         return lax.dot_general(
             slot_queries(slot), keys, (((1,), (1,)), ((), ())), preferred_element_type=F32
         )
@@ -124,8 +88,8 @@
         weights = jnp.where(live, jnp.exp(scores - top), 0.0)
         return top, jnp.sum(weights, axis=1, keepdims=True), weights.astype(BF)
 
-    def slot_values(slot, weights):
-        values = kv_scr[slot, :, :, kv_cols : 2 * kv_cols].reshape(tokens, kv_cols)
+    def slot_values(slot, ids, weights):
+        values = jnp.concatenate([pool_ref[i, :, kv_cols : 2 * kv_cols] for i in ids], axis=0)
         mixed = jnp.dot(weights, values, preferred_element_type=F32)
         folded = []
         for part in (mixed[:n_tp], mixed[n_tp:]):
@@ -139,12 +103,11 @@
     def some_slots(step, state):
         tops, sums = state
         group = [step * UNROLL + i for i in range(UNROLL)]
-        for slot in group:
-            wait_pages(slot)
-        scores = [slot_scores(slot) for slot in group]
+        ids = [[table_ref[slot, i] for i in range(pages)] for slot in group]
+        scores = [slot_scores(slot, i) for slot, i in zip(group, ids)]
         parts = [slot_weights(slot, s) for slot, s in zip(group, scores)]
-        for slot, (top, total, weights) in zip(group, parts):
-            slot_values(slot, weights)
+        for slot, i, (top, total, weights) in zip(group, ids, parts):
+            slot_values(slot, i, weights)
             here = lane == slot
             tops = jnp.where(here, top, tops)
             sums = jnp.where(here, total, sums)
@@ -165,15 +128,11 @@
         ).astype(BF)
 
 
-def combine_kernel(offsets, size_ref, msg_ref, q_ref, new_ref, *rest):
-    pair_refs, out_ref = rest[:-1], rest[-1]
+def merge_kernel(size_ref, msg_ref, q_ref, new_ref, out_ref):
     n_tp = msg_ref.shape[0]
     slots = q_ref.shape[0]
     live_count = size_ref[0]
     tp_index = axis_index("tp")
-    grp_index = axis_index("grp")
-    blocks = 2 * len(pair_refs)
-    width = pair_refs[0].shape[0] // 2
     ones_block = (
         lax.broadcasted_iota(jnp.int32, (LANES, LANES), 0) // HD
         == lax.broadcasted_iota(jnp.int32, (LANES, LANES), 1) // HD
@@ -226,9 +185,17 @@
     fresh = jnp.exp(self_score - final_top)
     attended = (numerator * cached + new_value * fresh) / (sum_all * cached + fresh)
     slot = lax.broadcasted_iota(jnp.int32, (slots, LANES), 0)
-    attended = jnp.where(slot < live_count, attended, 0.0).astype(BF)
-    parts = n_tp // blocks
-    rows = slots // parts
+    out_ref[...] = jnp.where(slot < live_count, attended, 0.0).astype(BF)
+
+
+def project_kernel(offsets, attended_ref, *rest):
+    pair_refs, out_ref = rest[:-1], rest[-1]
+    grp_index = axis_index("grp")
+    attended = attended_ref[...]
+    blocks = 2 * len(pair_refs)
+    width = pair_refs[0].shape[0] // 2
+    parts = out_ref.shape[0] // blocks
+    rows = attended.shape[0] // parts
     for offset, pair_ref in zip(offsets, pair_refs):
         for half in range(2):
             share = lax.dot_general(
@@ -242,8 +209,19 @@
                 out_ref[block * parts + i, :, 0:width] = share[i * rows : (i + 1) * rows]
 
 
-def copies_kernel(in_ref, out_ref):
+def rescale_kernel(in_ref, out_ref):
+    out_ref[...] = (in_ref[...].astype(F32) * HD**-0.5).reshape(out_ref.shape)
+
+
+def copies_kernel(size_ref, in_ref, out_ref):
+    del size_ref
     out_ref[...] = jnp.broadcast_to(in_ref[...][None], out_ref.shape)
+
+
+def join_kernel(one_ref, other_ref, out_ref):
+    rows = one_ref.shape[0]
+    out_ref[0:rows, :] = one_ref[...]
+    out_ref[rows : 2 * rows, :] = other_ref[...]
 
 
 def total_kernel(in_ref, out_ref):
@@ -282,52 +260,87 @@
     return jax.ShapeDtypeStruct(shape, dtype) if INTERPRET else pltpu.VMEM(shape, dtype)
 
 
-def copies(piece, count):
+def rescale(pieces):
+    return pl.pallas_call(
+        rescale_kernel,
+        out_shape=near_out((pieces.shape[0] * pieces.shape[1], pieces.shape[2]), F32),
+        in_specs=[VMEM()],
+        out_specs=VMEM(),
+        interpret=bool(INTERPRET),
+        compiler_params=PARAMS,
+        name="rescale",
+    )(near(pieces))
+
+
+def copies(sizes, piece, count):
     return pl.pallas_call(
         copies_kernel,
         out_shape=near_out((count, *piece.shape), piece.dtype),
-        in_specs=[VMEM()],
-        out_specs=VMEM(),
-        interpret=bool(INTERPRET),
-        compiler_params=PARAMS,
+        in_specs=[SMEM(), VMEM()],
+        out_specs=VMEM(),
+        interpret=bool(INTERPRET),
+        compiler_params=PARAMS,
+        cost_estimate=pl.CostEstimate(
+            flops=10**11, transcendentals=0, bytes_accessed=piece.size * 2 * (count + 1)
+        ),
         name="copies",
-    )(far(piece))
-
-
-def attend(sizes, lens, table, gathered, pool):
-    n_tp, slots, _ = gathered.shape
+    )(sizes, far(piece))
+
+
+def join(one, other):
+    return pl.pallas_call(
+        join_kernel,
+        out_shape=near_out((2 * one.shape[0], one.shape[1]), one.dtype),
+        in_specs=[VMEM()] * 2,
+        out_specs=VMEM(),
+        interpret=bool(INTERPRET),
+        compiler_params=PARAMS,
+        name="join",
+    )(near(one), near(other))
+
+
+def attend(sizes, lens, table, scaled, pool):
+    slots = table.shape[0]
+    n_tp = scaled.shape[0] // slots
     return pl.pallas_call(
         attend_kernel,
         out_shape=near_out((n_tp, MSG_ROWS, LANES), BF),
-        in_specs=[SMEM(), SMEM(), SMEM(), VMEM(), pl.BlockSpec(memory_space=pltpu.HBM)],
+        in_specs=[SMEM(), SMEM(), SMEM(), VMEM(), VMEM()],
         out_specs=VMEM(),
         scratch_shapes=[
-            pltpu.VMEM((slots, table.shape[1], *pool.shape[1:]), BF),
-            pltpu.VMEM((n_tp * slots, LANES), F32),
             pltpu.VMEM((slots * n_tp, LANES), F32),
             pltpu.VMEM((n_tp, LANES), F32),
-            pltpu.SemaphoreType.DMA((slots, table.shape[1] // CHUNK)),
         ],
         interpret=bool(INTERPRET),
         compiler_params=PARAMS,
         name="attend",
-    )(sizes, far(lens), far(table), near(gathered), far(pool))
-
-
-def combine(sizes, message, own, fresh, pairs):
-    n_tp = message.shape[0]
-    slots = own.shape[0]
-    rows = slots * 2 * len(pairs) // n_tp
+    )(sizes, far(lens), far(table), near(scaled), near(pool))
+
+
+def merge(sizes, message, own, fresh):
+    return pl.pallas_call(
+        merge_kernel,
+        out_shape=near_out(own.shape, BF),
+        in_specs=[SMEM()] + [VMEM()] * 3,
+        out_specs=VMEM(),
+        interpret=bool(INTERPRET),
+        compiler_params=PARAMS,
+        name="merge",
+    )(sizes, near(message), near(own), near(fresh))
+
+
+def project(attended, pairs, n_tp):
+    rows = attended.shape[0] * 2 * len(pairs) // n_tp
     width = -(-pairs[0].shape[0] // 2 // LANES) * LANES
     return pl.pallas_call(
-        functools.partial(combine_kernel, tuple(pairs)),
+        functools.partial(project_kernel, tuple(pairs)),
         out_shape=near_out((n_tp, rows, width), BF),
-        in_specs=[SMEM()] + [VMEM()] * (3 + len(pairs)),
-        out_specs=VMEM(),
-        interpret=bool(INTERPRET),
-        compiler_params=PARAMS,
-        name="combine",
-    )(sizes, near(message), near(own), near(fresh), *map(near, pairs.values()))
+        in_specs=[VMEM()] * (1 + len(pairs)),
+        out_specs=VMEM(),
+        interpret=bool(INTERPRET),
+        compiler_params=PARAMS,
+        name="project",
+    )(near(attended), *map(near, pairs.values()))
 
 
 def total_copies(pieces):
@@ -368,13 +381,17 @@
         return lax.ppermute(block, "grp", [(i, i ^ step) for i in range(n_grp)])
 
     own_block = out_weight.T
-    pair = jnp.concatenate([own_block, from_pair(own_block, FIRST_STEP)])
+    first = from_pair(own_block, FIRST_STEP)
+    fanned = copies(batch_sizes, own, n_tp)
+    gathered = exchange(fanned, "tp")
+    scaled = rescale(gathered)
+    late_block, scaled = lax.optimization_barrier((own_block, scaled))
+    pair = join(late_block, first)
     pairs = {0: pair, **{step: from_pair(pair, step) for step in PAIR_STEPS}}
-    fanned = copies(own, n_tp)
-    gathered = exchange(fanned, "tp")
-    message = attend(batch_sizes, seq_lens[0], page_table[0], gathered, kv_pool[0])
+    message = attend(batch_sizes, seq_lens[0], page_table[0], scaled, kv_pool[0])
     received = exchange(message, "tp")
-    shares = combine(batch_sizes, received, own, new_kv[0], pairs)
+    attended = merge(batch_sizes, received, own, new_kv[0])
+    shares = project(attended, pairs, n_tp)
     totals = total_copies(exchange(shares, "tp"))
     return finish(exchange(totals, "tp"), slots, n_grp * out_weight.shape[1])
 

time: 87 us -> 91 us (1.046)
  blocking collectives: 34.7 us -> 59.6 us
  starting transfers between devices: 25.8 us -> 13.3 us
  waiting for transfers between devices: 17.7 us -> 11.6 us
  Pallas kernels: 7.52 us -> 5.36 us
    all_to_all x2 -> x3, blocking collectives: 34.7 us -> 59.6 us  [exchange(): return lax.all_to_all(pieces, axis, split_axis=0, concat_axis=0, tiled=True)]
    all_to_all x2 -> x1, starting transfers between devices: 17.8 us -> 5.19 us  [exchange(): return lax.all_to_all(pieces, axis, split_axis=0, concat_axis=0, tiled=True)]
    all_to_all x2 -> x1, waiting for transfers between devices: 9.45 us -> 0.01 us  [exchange(): return lax.all_to_all(pieces, axis, split_axis=0, concat_axis=0, tiled=True)]
    ppermute x4, waiting for transfers between devices: 8.24 us -> 11.6 us  [from_pair(): return lax.ppermute(block, 'grp', [(i, i ^ step) for i in range(n_grp)])]
    pallas_call x1, Pallas kernels: 4.57 us -> 2.97 us  [attend(): pl.pallas_call(attend_kernel, out_shape=near_out((n_tp, MSG_ROWS, LANES),...]
  transfers between devices with their start and end apart: 6 -> 5, of which waited for: 3 -> 3; matrix products, arithmetic and copies ran while one was open for 0% -> 0% of each run, Pallas kernels for 5% -> 0%
where the time goes in v3:
time: 91 us; the launch traced here: 90.6 us
  blocking collectives  59.6 us (65%)
  starting transfers between devices  13.3 us (15%)
  waiting for transfers between devices  11.6 us (13%)
  Pallas kernels  5.36 us (6%)
    all_to_all x3, blocking collectives, exchange(): return lax.all_to_all(pieces, axis, split_axis=0, concat_axis=0, tiled=True)  59.6 us
    ppermute x4, waiting for transfers between devices, from_pair(): return lax.ppermute(block, 'grp', [(i, i ^ step) for i in range(n_grp)])  11.6 us
    ppermute x4, starting transfers between devices, from_pair(): return lax.ppermute(block, 'grp', [(i, i ^ step) for i in range(n_grp)])  8.06 us
    all_to_all x1, starting transfers between devices, exchange(): return lax.all_to_all(pieces, axis, split_axis=0, concat_axis=0, tiled=True)  5.19 us
    pallas_call x1, Pallas kernels, attend(): pl.pallas_call(attend_kernel, out_shape=near_out((n_tp, MSG_ROWS, LANES),...  2.97 us
  transfers between devices with their start and end apart: 5, of which 3 were waited for; matrix products, arithmetic and copies ran while one was open for 0% of the time, Pallas kernels for 0%

profile of v3, /device:TPU:1, one launch (start us, length us, event | category | flops | bytes accessed | tf_op | source)
XLA Modules:
  0.0 90.6 jit_solution(1593546692076698833)
XLA Ops:
  0.7 0.0 copy-start
  0.7 0.9 copies.1
  1.5 0.0 copy-start.1
  1.5 0.0 copy-start.2
  1.5 0.0 copy-start.3
  1.6 23.1 %all_to_all.20.in_ref = bf16[32,16,128]{2,1,0:T(8,128)(2,1)S(1)} all-to-all(bf16[32,16,128]{2,1,0:T(8,128)(2,1)S(1)} %copies.1), channel_id=1, replica_groups=mesh['grp'=8,'tp'=32] {'tp'}, dimensions={0} | all-to-all | bytes 262144 | tf_op jit(solution)/shard_map/all_to_all | solution.py:371
  24.7 0.0 copy-done
  24.7 3.0 %attend.1 = bf16[32,24,128]{2,1,0:T(8,128)(2,1)} custom-call(s32[1]{0:T(128)S(6)} %copy.8.size_ref, s32[16]{0:T(128)} %bitcast.13, s32[16,16]{1,0:T(8,128)} %bitcast.12, f32[512,128]{1,0:T(8,128)S(1)} %rescale.1.q_ref, bf16[256,16,1024]{2,1,0:T(8,128)(2,1)S(1)} %bitcast.6), custom_call_target="tpu_custom_call" | custom-call | tf_op jit(solution)/shard_map/attend/pallas_call | solution.py:305
  27.7 5.2 %all-to-all-start.1 = ((bf16[32,24,128]{2,1,0:T(8,128)(2,1)}), bf16[32,24,128]{2,1,0:T(8,128)(2,1)S(1)}, u32[]{:S(2)}, u32[]{:S(2)}) async-start(bf16[32,24,128]{2,1,0:T(8,128)(2,1)} %attend.1), calls=%async_computation.1 | async-start | bytes 393216 | tf_op jit(solution)/shard_map/all_to_all | solution.py:371
  32.9 0.0 copy-done.1
  32.9 0.4 collective-permute-start
  33.3 4.0 %collective-permute-done.other_ref = bf16[360,128]{1,0:T(8,128)(2,1)S(1)} collective-permute-done((bf16[360,128]{1,0:T(8,128)(2,1)S(1)}, bf16[360,128]{1,0:T(8,128)(2,1)S(1)}, u32[]{:S(2)}, u32[]{:S(2)}) %collective-permute-start) | collective-permute-done | bytes 92192 | tf_op jit(solution)/shard_map/ppermute | solution.py:381
  37.3 4.3 %collective-permute-start.3 = (bf16[720,128]{1,0:T(8,128)(2,1)S(1)}, bf16[720,128]{1,0:T(8,128)(2,1)S(1)}, u32[]{:S(2)}, u32[]{:S(2)}) collective-permute-start(bf16[720,128]{1,0:T(8,128)(2,1)S(1)} %join.1.rest_0_), channel_id=1, source_target_pairs={{0,32},{32,0},{64,96},{96,64},{128,160},{160,128},{192,224},{224,1... | collective-permute-start | bytes 552968 | tf_op jit(solution)/shard_map/ppermute | solution.py:381
  41.6 3.4 %collective-permute-start.2 = (bf16[720,128]{1,0:T(8,128)(2,1)S(1)}, bf16[720,128]{1,0:T(8,128)(2,1)S(1)}, u32[]{:S(2)}, u32[]{:S(2)}) collective-permute-start(bf16[720,128]{1,0:T(8,128)(2,1)S(1)} %join.1.rest_0_), channel_id=1, source_target_pairs={{0,96},{32,64},{64,32},{96,0},{128,224},{160,192},{192,160},{224,1... | collective-permute-start | bytes 552968 | tf_op jit(solution)/shard_map/ppermute | solution.py:381
  44.9 0.0 collective-permute-start.1
  44.9 0.0 all-to-all-done.1.msg_ref
  45.0 0.3 merge.1.attended_ref
  45.3 0.2 collective-permute-done.3.rest_3_
  45.5 7.5 %collective-permute-done.2.rest_2_ = bf16[720,128]{1,0:T(8,128)(2,1)S(1)} collective-permute-done((bf16[720,128]{1,0:T(8,128)(2,1)S(1)}, bf16[720,128]{1,0:T(8,128)(2,1)S(1)}, u32[]{:S(2)}, u32[]{:S(2)}) %collective-permute-start.2) | collective-permute-done | bytes 184352 | tf_op jit(solution)/shard_map/ppermute | solution.py:381
  52.9 0.0 collective-permute-done.1.rest_1_
  52.9 0.4 project.1
  53.3 22.3 %all_to_all.21.in_ref = bf16[32,4,384]{2,1,0:T(4,128)(2,1)S(1)} all-to-all(bf16[32,4,384]{2,1,0:T(4,128)(2,1)S(1)} %project.1), channel_id=1, replica_groups=mesh['grp'=8,'tp'=32] {'tp'}, dimensions={0} | all-to-all | bytes 196608 | tf_op jit(solution)/shard_map/all_to_all | solution.py:371
  75.6 14.2 %all_to_all.22.in_ref = bf16[32,4,384]{2,1,0:T(4,128)(2,1)S(1)} all-to-all(bf16[32,4,384]{2,1,0:T(4,128)(2,1)S(1)} %total.1), channel_id=1, replica_groups=mesh['grp'=8,'tp'=32] {'tp'}, dimensions={0} | all-to-all | bytes 196608 | tf_op jit(solution)/shard_map/all_to_all | solution.py:371
  89.8 0.8 finish.1
  (5 shorter events, 0.1 us)
Async XLA Ops:
  0.7 24.1 %copy-start = (bf16[1,256,16,1024]{3,2,1,0:T(8,128)(2,1)S(1)}, bf16[1,256,16,1024]{3,2,1,0:T(8,128)(2,1)}, u32[]{:S(2)}) copy-start(bf16[1,256,16,1024]{3,2,1,0:T(8,128)(2,1)} %param.11) | copy-start | bytes 25165828
  1.5 31.4 %copy-start.1 = (bf16[128,360]{0,1:T(8,128)(2,1)S(1)}, bf16[128,360]{0,1:T(8,128)(2,1)}, u32[]{:S(2)}) copy-start(bf16[128,360]{0,1:T(8,128)(2,1)} %param.13) | copy-start | bytes 276484
  1.5 43.4 %copy-start.2 = (bf16[1,16,1024]{2,1,0:T(8,128)(2,1)S(1)}, bf16[1,16,1024]{2,1,0:T(8,128)(2,1)}, u32[]{:S(2)}) copy-start(bf16[1,16,1024]{2,1,0:T(8,128)(2,1)} %param.12) | copy-start | bytes 98308
  1.5 43.4 %copy-start.3 = (bf16[1,16,128]{2,1,0:T(8,128)(2,1)S(1)}, bf16[1,16,128]{2,1,0:T(8,128)(2,1)}, u32[]{:S(2)}) copy-start(bf16[1,16,128]{2,1,0:T(8,128)(2,1)} %param.10) | copy-start | bytes 12292
  27.7 17.2 %all-to-all-start.1 = ((bf16[32,24,128]{2,1,0:T(8,128)(2,1)}), bf16[32,24,128]{2,1,0:T(8,128)(2,1)S(1)}, u32[]{:S(2)}, u32[]{:S(2)}) async-start(bf16[32,24,128]{2,1,0:T(8,128)(2,1)} %attend.1), calls=%async_computation.1 | async-start | bytes 393216 | tf_op jit(solution)/shard_map/all_to_all | solution.py:371
  32.9 4.4 %collective-permute-start = (bf16[360,128]{1,0:T(8,128)(2,1)S(1)}, bf16[360,128]{1,0:T(8,128)(2,1)S(1)}, u32[]{:S(2)}, u32[]{:S(2)}) collective-permute-start(bf16[360,128]{1,0:T(8,128)(2,1)S(1)} %bitcast.7), channel_id=1, source_target_pairs={{0,128},{32,160},{64,192},{96,224},{128,0},{160,32},{192,64},{224,... | collective-permute-start | bytes 276488 | tf_op jit(solution)/shard_map/ppermute | solution.py:381
  37.3 8.2 %collective-permute-start.3 = (bf16[720,128]{1,0:T(8,128)(2,1)S(1)}, bf16[720,128]{1,0:T(8,128)(2,1)S(1)}, u32[]{:S(2)}, u32[]{:S(2)}) collective-permute-start(bf16[720,128]{1,0:T(8,128)(2,1)S(1)} %join.1.rest_0_), channel_id=1, source_target_pairs={{0,32},{32,0},{64,96},{96,64},{128,160},{160,128},{192,224},{224,1... | collective-permute-start | bytes 552968 | tf_op jit(solution)/shard_map/ppermute | solution.py:381
  41.6 11.4 %collective-permute-start.2 = (bf16[720,128]{1,0:T(8,128)(2,1)S(1)}, bf16[720,128]{1,0:T(8,128)(2,1)S(1)}, u32[]{:S(2)}, u32[]{:S(2)}) collective-permute-start(bf16[720,128]{1,0:T(8,128)(2,1)S(1)} %join.1.rest_0_), channel_id=1, source_target_pairs={{0,96},{32,64},{64,32},{96,0},{128,224},{160,192},{192,160},{224,1... | collective-permute-start | bytes 552968 | tf_op jit(solution)/shard_map/ppermute | solution.py:381
  44.9 8.0 %collective-permute-start.1 = (bf16[720,128]{1,0:T(8,128)(2,1)S(1)}, bf16[720,128]{1,0:T(8,128)(2,1)S(1)}, u32[]{:S(2)}, u32[]{:S(2)}) collective-permute-start(bf16[720,128]{1,0:T(8,128)(2,1)S(1)} %join.1.rest_0_), channel_id=1, source_target_pairs={{0,64},{32,96},{64,0},{96,32},{128,192},{160,224},{192,128},{224,1... | collective-permute-start | bytes 552968 | tf_op jit(solution)/shard_map/ppermute | solution.py:381

commit v4 on v2

--- a/solution.py
+++ b/solution.py
@@ -20,8 +20,8 @@
 INTERPRET = False
 FIRST_STEP = 4
 PAIR_STEPS = (2, 3, 1)
-UNROLL = 2
-CHUNK = 4
+UNROLL = 4
+CHUNK = 16
 
 
 def axis_index(name):
@@ -91,7 +91,9 @@
                 ).wait()
 
     lax.fori_loop(0, steps * UNROLL, lambda slot, _: load_pages(slot), None)
-    q_scr[...] = (q_ref[...].astype(F32) * HD**-0.5).reshape(n_tp * slots, LANES)
+    pad = slots + 1
+    for t in range(n_tp):
+        q_scr[t * pad : t * pad + slots, :] = q_ref[t].astype(F32) * HD**-0.5
     num_scr[...] = jnp.zeros_like(num_scr)
     low_half = lane_iota(n_tp) < HD
     own_block = (
@@ -103,7 +105,7 @@
     lane = lane_iota(HEADS)
 
     def slot_queries(slot):
-        x = q_scr[pl.ds(slot, n_tp, stride=slots), :]
+        x = q_scr[pl.ds(slot, n_tp, stride=pad), :]
         turned = roll_lanes(x, HD)
         even = jnp.where(low_half, x, turned)
         odd = jnp.where(low_half, turned, x)
@@ -132,7 +134,7 @@
             part = jnp.where(own_block, part, 0.0)
             part = sum(part[:, i * LANES : (i + 1) * LANES] for i in range(4))
             folded.append(part + roll_lanes(part, HD))
-        num_scr[pl.ds(pl.multiple_of(slot * n_tp, n_tp), n_tp), :] = jnp.where(
+        num_scr[pl.ds(slot * (n_tp + 1), n_tp), :] = jnp.where(
             low_half, folded[0], folded[1]
         )
 
@@ -159,7 +161,7 @@
     packed = tops + roll_lanes(hi.astype(F32), slots) + roll_lanes(lo.astype(F32), 2 * slots)
     stat_scr[...] = packed[:n_tp] + roll_lanes(packed[n_tp:], HD)
     for t in range(n_tp):
-        out_ref[t, 0:slots, :] = num_scr[pl.ds(t, slots, stride=n_tp), :].astype(BF)
+        out_ref[t, 0:slots, :] = num_scr[pl.ds(t, slots, stride=n_tp + 1), :].astype(BF)
         out_ref[t, STAT_ROW:MSG_ROWS, :] = jnp.broadcast_to(
             stat_scr[t : t + 1, :], (MSG_ROWS - STAT_ROW, LANES)
         ).astype(BF)
@@ -246,6 +248,12 @@
     out_ref[...] = jnp.broadcast_to(in_ref[...][None], out_ref.shape)
 
 
+def join_kernel(one_ref, other_ref, out_ref):
+    rows = one_ref.shape[0]
+    out_ref[0:rows, :] = one_ref[...]
+    out_ref[rows : 2 * rows, :] = other_ref[...]
+
+
 def total_kernel(in_ref, out_ref):
     n_tp = in_ref.shape[0]
     total = sum(in_ref[t].astype(F32) for t in range(n_tp)).astype(BF)
@@ -290,8 +298,23 @@
         out_specs=VMEM(),
         interpret=bool(INTERPRET),
         compiler_params=PARAMS,
+        cost_estimate=pl.CostEstimate(
+            flops=10**11, transcendentals=0, bytes_accessed=piece.size * 2 * (count + 1)
+        ),
         name="copies",
     )(far(piece))
+
+
+def join(one, other):
+    return pl.pallas_call(
+        join_kernel,
+        out_shape=near_out((2 * one.shape[0], one.shape[1]), one.dtype),
+        in_specs=[VMEM()] * 2,
+        out_specs=VMEM(),
+        interpret=bool(INTERPRET),
+        compiler_params=PARAMS,
+        name="join",
+    )(near(one), near(other))
 
 
 def attend(sizes, lens, table, gathered, pool):
@@ -303,8 +326,8 @@
         out_specs=VMEM(),
         scratch_shapes=[
             pltpu.VMEM((slots, table.shape[1], *pool.shape[1:]), BF),
-            pltpu.VMEM((n_tp * slots, LANES), F32),
-            pltpu.VMEM((slots * n_tp, LANES), F32),
+            pltpu.VMEM((n_tp * (slots + 1), LANES), F32),
+            pltpu.VMEM((slots * (n_tp + 1), LANES), F32),
             pltpu.VMEM((n_tp, LANES), F32),
             pltpu.SemaphoreType.DMA((slots, table.shape[1] // CHUNK)),
         ],
@@ -368,7 +391,7 @@
         return lax.ppermute(block, "grp", [(i, i ^ step) for i in range(n_grp)])
 
     own_block = out_weight.T
-    pair = jnp.concatenate([own_block, from_pair(own_block, FIRST_STEP)])
+    pair = join(own_block, from_pair(own_block, FIRST_STEP))
     pairs = {0: pair, **{step: from_pair(pair, step) for step in PAIR_STEPS}}
     fanned = copies(own, n_tp)
     gathered = exchange(fanned, "tp")

time: 87 us -> 91.1 us (1.047)
  waiting for transfers between devices: 17.7 us -> 21.9 us
  blocking collectives: 34.7 us -> 36.5 us
  starting transfers between devices: 25.8 us -> 24.5 us
    ppermute x4, waiting for transfers between devices: 8.24 us -> 12 us  [from_pair(): return lax.ppermute(block, 'grp', [(i, i ^ step) for i in range(n_grp)])]
    all_to_all x2, blocking collectives: 34.7 us -> 36.5 us  [exchange(): return lax.all_to_all(pieces, axis, split_axis=0, concat_axis=0, tiled=True)]
    ppermute x4, starting transfers between devices: 8.01 us -> 6.58 us  [from_pair(): return lax.ppermute(block, 'grp', [(i, i ^ step) for i in range(n_grp)])]
  transfers between devices with their start and end apart: 6 -> 6, of which waited for: 3 -> 4; matrix products, arithmetic and copies ran while one was open for 0% -> 0% of each run, Pallas kernels for 5% -> 0%
where the time goes in v4:
time: 91.1 us; the launch traced here: 90.6 us
  blocking collectives  36.5 us (40%)
  starting transfers between devices  24.5 us (27%)
  waiting for transfers between devices  21.9 us (24%)
  Pallas kernels  6.98 us (8%)
    all_to_all x2, blocking collectives, exchange(): return lax.all_to_all(pieces, axis, split_axis=0, concat_axis=0, tiled=True)  36.5 us
    all_to_all x2, starting transfers between devices, exchange(): return lax.all_to_all(pieces, axis, split_axis=0, concat_axis=0, tiled=True)  17.9 us
    ppermute x4, waiting for transfers between devices, from_pair(): return lax.ppermute(block, 'grp', [(i, i ^ step) for i in range(n_grp)])  12 us
    all_to_all x2, waiting for transfers between devices, exchange(): return lax.all_to_all(pieces, axis, split_axis=0, concat_axis=0, tiled=True)  9.85 us
    ppermute x4, starting transfers between devices, from_pair(): return lax.ppermute(block, 'grp', [(i, i ^ step) for i in range(n_grp)])  6.58 us
    pallas_call x1, Pallas kernels, attend(): pl.pallas_call(attend_kernel, out_shape=near_out((n_tp, MSG_ROWS, LANES),...  4.07 us
  transfers between devices with their start and end apart: 6, of which 4 were waited for; matrix products, arithmetic and copies ran while one was open for 0% of the time, Pallas kernels for 0%

profile of v4, /device:TPU:1, one launch (start us, length us, event | category | flops | bytes accessed | tf_op | source)
XLA Modules:
  0.0 90.6 jit_solution(11903866617253340230)
XLA Ops:
  0.0 1.4 %copies.1 = bf16[32,16,128]{2,1,0:T(8,128)(2,1)} custom-call(bf16[16,128]{1,0:T(8,128)(2,1)} %bitcast.9), custom_call_target="tpu_custom_call" | custom-call | flops 99999997952 | bytes 135168 | tf_op jit(solution)/shard_map/copies/pallas_call | solution.py:294
  1.4 0.0 copy-start
  1.4 0.0 copy-start.1
  1.4 0.0 copy-start.2
  1.4 12.7 %all-to-all-start = ((bf16[32,16,128]{2,1,0:T(8,128)(2,1)}), bf16[32,16,128]{2,1,0:T(8,128)(2,1)S(1)}, u32[]{:S(2)}, u32[]{:S(2)}) async-start(bf16[32,16,128]{2,1,0:T(8,128)(2,1)} %copies.1), calls=%async_computation | async-start | bytes 262144 | tf_op jit(solution)/shard_map/all_to_all | solution.py:381
  14.7 9.9 %all-to-all-done.q_ref = bf16[32,16,128]{2,1,0:T(8,128)(2,1)S(1)} async-done(((bf16[32,16,128]{2,1,0:T(8,128)(2,1)}), bf16[32,16,128]{2,1,0:T(8,128)(2,1)S(1)}, u32[]{:S(2)}, u32[]{:S(2)}) %all-to-all-start) | async-done | bytes 131104 | tf_op jit(solution)/shard_map/all_to_all | solution.py:381
  24.6 4.1 %attend.1 = bf16[32,24,128]{2,1,0:T(8,128)(2,1)} custom-call(s32[1]{0:T(128)S(6)} %copy.8.size_ref, s32[16]{0:T(128)} %bitcast.13, s32[16,16]{1,0:T(8,128)} %bitcast.12, bf16[32,16,128]{2,1,0:T(8,128)(2,1)S(1)} %all-to-all-done.q_ref, bf16[256,16,1024]{2,1,0:T(8,128)(2,1)} %bitcast.11), custom_call_target="tpu_custom_call" | custom-call | tf_op jit(solution)/shard_map/attend/pallas_call | solution.py:322
  28.7 5.2 %all-to-all-start.1 = ((bf16[32,24,128]{2,1,0:T(8,128)(2,1)}), bf16[32,24,128]{2,1,0:T(8,128)(2,1)S(1)}, u32[]{:S(2)}, u32[]{:S(2)}) async-start(bf16[32,24,128]{2,1,0:T(8,128)(2,1)} %attend.1), calls=%async_computation.1 | async-start | bytes 393216 | tf_op jit(solution)/shard_map/all_to_all | solution.py:381
  33.9 0.0 copy-done
  33.9 0.2 collective-permute-start
  34.1 4.1 %collective-permute-done.other_ref = bf16[360,128]{1,0:T(8,128)(2,1)S(1)} collective-permute-done((bf16[360,128]{1,0:T(8,128)(2,1)S(1)}, bf16[360,128]{1,0:T(8,128)(2,1)S(1)}, u32[]{:S(2)}, u32[]{:S(2)}) %collective-permute-start) | collective-permute-done | bytes 92192 | tf_op jit(solution)/shard_map/ppermute | solution.py:391
  38.2 3.0 %collective-permute-start.3 = (bf16[720,128]{1,0:T(8,128)(2,1)S(1)}, bf16[720,128]{1,0:T(8,128)(2,1)S(1)}, u32[]{:S(2)}, u32[]{:S(2)}) collective-permute-start(bf16[720,128]{1,0:T(8,128)(2,1)S(1)} %join.1.rest_0_), channel_id=1, source_target_pairs={{0,32},{32,0},{64,96},{96,64},{128,160},{160,128},{192,224},{224,1... | collective-permute-start | bytes 552968 | tf_op jit(solution)/shard_map/ppermute | solution.py:391
  41.2 3.3 %collective-permute-start.2 = (bf16[720,128]{1,0:T(8,128)(2,1)S(1)}, bf16[720,128]{1,0:T(8,128)(2,1)S(1)}, u32[]{:S(2)}, u32[]{:S(2)}) collective-permute-start(bf16[720,128]{1,0:T(8,128)(2,1)S(1)} %join.1.rest_0_), channel_id=1, source_target_pairs={{0,96},{32,64},{64,32},{96,0},{128,224},{160,192},{192,160},{224,1... | collective-permute-start | bytes 552968 | tf_op jit(solution)/shard_map/ppermute | solution.py:391
  44.5 0.0 collective-permute-start.1
  44.5 0.5 collective-permute-done.3.rest_3_
  45.1 7.4 %collective-permute-done.2.rest_2_ = bf16[720,128]{1,0:T(8,128)(2,1)S(1)} collective-permute-done((bf16[720,128]{1,0:T(8,128)(2,1)S(1)}, bf16[720,128]{1,0:T(8,128)(2,1)S(1)}, u32[]{:S(2)}, u32[]{:S(2)}) %collective-permute-start.2) | collective-permute-done | bytes 184352 | tf_op jit(solution)/shard_map/ppermute | solution.py:391
  52.5 0.0 collective-permute-done.1.rest_1_
  52.5 0.0 all-to-all-done.1.msg_ref
  52.5 0.0 copy-done.1
  52.5 0.0 copy-done.2
  52.5 0.7 combine.1
  53.2 22.3 %all_to_all.20.in_ref = bf16[32,4,384]{2,1,0:T(4,128)(2,1)S(1)} all-to-all(bf16[32,4,384]{2,1,0:T(4,128)(2,1)S(1)} %combine.1), channel_id=1, replica_groups=mesh['grp'=8,'tp'=32] {'tp'}, dimensions={0} | all-to-all | bytes 196608 | tf_op jit(solution)/shard_map/all_to_all | solution.py:381
  75.6 14.2 %all_to_all.21.in_ref = bf16[32,4,384]{2,1,0:T(4,128)(2,1)S(1)} all-to-all(bf16[32,4,384]{2,1,0:T(4,128)(2,1)S(1)} %total.1), channel_id=1, replica_groups=mesh['grp'=8,'tp'=32] {'tp'}, dimensions={0} | all-to-all | bytes 196608 | tf_op jit(solution)/shard_map/all_to_all | solution.py:381
  89.8 0.8 finish.1
  (2 shorter events, 0.1 us)
Async XLA Ops:
  1.4 32.5 %copy-start = (bf16[128,360]{0,1:T(8,128)(2,1)S(1)}, bf16[128,360]{0,1:T(8,128)(2,1)}, u32[]{:S(2)}) copy-start(bf16[128,360]{0,1:T(8,128)(2,1)} %param.13) | copy-start | bytes 276484
  1.4 51.2 %copy-start.1 = (bf16[1,16,1024]{2,1,0:T(8,128)(2,1)S(1)}, bf16[1,16,1024]{2,1,0:T(8,128)(2,1)}, u32[]{:S(2)}) copy-start(bf16[1,16,1024]{2,1,0:T(8,128)(2,1)} %param.12) | copy-start | bytes 98308
  1.4 51.2 %copy-start.2 = (bf16[1,16,128]{2,1,0:T(8,128)(2,1)S(1)}, bf16[1,16,128]{2,1,0:T(8,128)(2,1)}, u32[]{:S(2)}) copy-start(bf16[1,16,128]{2,1,0:T(8,128)(2,1)} %param.10) | copy-start | bytes 12292
  1.4 23.2 %all-to-all-start = ((bf16[32,16,128]{2,1,0:T(8,128)(2,1)}), bf16[32,16,128]{2,1,0:T(8,128)(2,1)S(1)}, u32[]{:S(2)}, u32[]{:S(2)}) async-start(bf16[32,16,128]{2,1,0:T(8,128)(2,1)} %copies.1), calls=%async_computation | async-start | bytes 262144 | tf_op jit(solution)/shard_map/all_to_all | solution.py:381
  28.7 23.9 %all-to-all-start.1 = ((bf16[32,24,128]{2,1,0:T(8,128)(2,1)}), bf16[32,24,128]{2,1,0:T(8,128)(2,1)S(1)}, u32[]{:S(2)}, u32[]{:S(2)}) async-start(bf16[32,24,128]{2,1,0:T(8,128)(2,1)} %attend.1), calls=%async_computation.1 | async-start | bytes 393216 | tf_op jit(solution)/shard_map/all_to_all | solution.py:381
  33.9 4.3 %collective-permute-start = (bf16[360,128]{1,0:T(8,128)(2,1)S(1)}, bf16[360,128]{1,0:T(8,128)(2,1)S(1)}, u32[]{:S(2)}, u32[]{:S(2)}) collective-permute-start(bf16[360,128]{1,0:T(8,128)(2,1)S(1)} %bitcast.6), channel_id=1, source_target_pairs={{0,128},{32,160},{64,192},{96,224},{128,0},{160,32},{192,64},{224,... | collective-permute-start | bytes 276488 | tf_op jit(solution)/shard_map/ppermute | solution.py:391
  38.2 6.9 %collective-permute-start.3 = (bf16[720,128]{1,0:T(8,128)(2,1)S(1)}, bf16[720,128]{1,0:T(8,128)(2,1)S(1)}, u32[]{:S(2)}, u32[]{:S(2)}) collective-permute-start(bf16[720,128]{1,0:T(8,128)(2,1)S(1)} %join.1.rest_0_), channel_id=1, source_target_pairs={{0,32},{32,0},{64,96},{96,64},{128,160},{160,128},{192,224},{224,1... | collective-permute-start | bytes 552968 | tf_op jit(solution)/shard_map/ppermute | solution.py:391
  41.2 11.3 %collective-permute-start.2 = (bf16[720,128]{1,0:T(8,128)(2,1)S(1)}, bf16[720,128]{1,0:T(8,128)(2,1)S(1)}, u32[]{:S(2)}, u32[]{:S(2)}) collective-permute-start(bf16[720,128]{1,0:T(8,128)(2,1)S(1)} %join.1.rest_0_), channel_id=1, source_target_pairs={{0,96},{32,64},{64,32},{96,0},{128,224},{160,192},{192,160},{224,1... | collective-permute-start | bytes 552968 | tf_op jit(solution)/shard_map/ppermute | solution.py:391
  44.5 8.0 %collective-permute-start.1 = (bf16[720,128]{1,0:T(8,128)(2,1)S(1)}, bf16[720,128]{1,0:T(8,128)(2,1)S(1)}, u32[]{:S(2)}, u32[]{:S(2)}) collective-permute-start(bf16[720,128]{1,0:T(8,128)(2,1)S(1)} %join.1.rest_0_), channel_id=1, source_target_pairs={{0,64},{32,96},{64,0},{96,32},{128,192},{160,224},{192,128},{224,1... | collective-permute-start | bytes 552968 | tf_op jit(solution)/shard_map/ppermute | solution.py:391

commit v5 on v4

--- a/solution.py
+++ b/solution.py
@@ -167,15 +167,11 @@
         ).astype(BF)
 
 
-def combine_kernel(offsets, size_ref, msg_ref, q_ref, new_ref, *rest):
-    pair_refs, out_ref = rest[:-1], rest[-1]
+def merge_kernel(size_ref, msg_ref, q_ref, new_ref, out_ref):
     n_tp = msg_ref.shape[0]
     slots = q_ref.shape[0]
     live_count = size_ref[0]
     tp_index = axis_index("tp")
-    grp_index = axis_index("grp")
-    blocks = 2 * len(pair_refs)
-    width = pair_refs[0].shape[0] // 2
     ones_block = (
         lax.broadcasted_iota(jnp.int32, (LANES, LANES), 0) // HD
         == lax.broadcasted_iota(jnp.int32, (LANES, LANES), 1) // HD
@@ -228,9 +224,17 @@
     fresh = jnp.exp(self_score - final_top)
     attended = (numerator * cached + new_value * fresh) / (sum_all * cached + fresh)
     slot = lax.broadcasted_iota(jnp.int32, (slots, LANES), 0)
-    attended = jnp.where(slot < live_count, attended, 0.0).astype(BF)
-    parts = n_tp // blocks
-    rows = slots // parts
+    out_ref[...] = jnp.where(slot < live_count, attended, 0.0).astype(BF)
+
+
+def project_kernel(offsets, attended_ref, *rest):
+    pair_refs, out_ref = rest[:-1], rest[-1]
+    grp_index = axis_index("grp")
+    attended = attended_ref[...]
+    blocks = 2 * len(pair_refs)
+    width = pair_refs[0].shape[0] // 2
+    parts = out_ref.shape[0] // blocks
+    rows = attended.shape[0] // parts
     for offset, pair_ref in zip(offsets, pair_refs):
         for half in range(2):
             share = lax.dot_general(
@@ -337,20 +341,30 @@
     )(sizes, far(lens), far(table), near(gathered), far(pool))
 
 
-def combine(sizes, message, own, fresh, pairs):
-    n_tp = message.shape[0]
-    slots = own.shape[0]
-    rows = slots * 2 * len(pairs) // n_tp
+def merge(sizes, message, own, fresh):
+    return pl.pallas_call(
+        merge_kernel,
+        out_shape=near_out(own.shape, BF),
+        in_specs=[SMEM()] + [VMEM()] * 3,
+        out_specs=VMEM(),
+        interpret=bool(INTERPRET),
+        compiler_params=PARAMS,
+        name="merge",
+    )(sizes, near(message), near(own), near(fresh))
+
+
+def project(attended, pairs, n_tp):
+    rows = attended.shape[0] * 2 * len(pairs) // n_tp
     width = -(-pairs[0].shape[0] // 2 // LANES) * LANES
     return pl.pallas_call(
-        functools.partial(combine_kernel, tuple(pairs)),
+        functools.partial(project_kernel, tuple(pairs)),
         out_shape=near_out((n_tp, rows, width), BF),
-        in_specs=[SMEM()] + [VMEM()] * (3 + len(pairs)),
-        out_specs=VMEM(),
-        interpret=bool(INTERPRET),
-        compiler_params=PARAMS,
-        name="combine",
-    )(sizes, near(message), near(own), near(fresh), *map(near, pairs.values()))
+        in_specs=[VMEM()] * (1 + len(pairs)),
+        out_specs=VMEM(),
+        interpret=bool(INTERPRET),
+        compiler_params=PARAMS,
+        name="project",
+    )(near(attended), *map(near, pairs.values()))
 
 
 def total_copies(pieces):
@@ -397,7 +411,8 @@
     gathered = exchange(fanned, "tp")
     message = attend(batch_sizes, seq_lens[0], page_table[0], gathered, kv_pool[0])
     received = exchange(message, "tp")
-    shares = combine(batch_sizes, received, own, new_kv[0], pairs)
+    attended = merge(batch_sizes, received, own, new_kv[0])
+    shares = project(attended, pairs, n_tp)
     totals = total_copies(exchange(shares, "tp"))
     return finish(exchange(totals, "tp"), slots, n_grp * out_weight.shape[1])
 

time: 91.1 us -> 90.7 us (level)
    ppermute x4, waiting for transfers between devices: 12 us -> 10.6 us  [from_pair(): return lax.ppermute(block, 'grp', [(i, i ^ step) for i in range(n_grp)])]
    all_to_all x2, waiting for transfers between devices: 9.85 us -> 10.9 us  [exchange(): return lax.all_to_all(pieces, axis, split_axis=0, concat_axis=0, tiled=True)]
where the time goes in v5:
time: 90.7 us; the launch traced here: 90.2 us
  blocking collectives  36.5 us (40%)
  starting transfers between devices  24.5 us (27%)
  waiting for transfers between devices  21.6 us (24%)
  Pallas kernels  6.94 us (8%)
    all_to_all x2, blocking collectives, exchange(): return lax.all_to_all(pieces, axis, split_axis=0, concat_axis=0, tiled=True)  36.5 us
    all_to_all x2, starting transfers between devices, exchange(): return lax.all_to_all(pieces, axis, split_axis=0, concat_axis=0, tiled=True)  17.9 us
    all_to_all x2, waiting for transfers between devices, exchange(): return lax.all_to_all(pieces, axis, split_axis=0, concat_axis=0, tiled=True)  10.9 us
    ppermute x4, waiting for transfers between devices, from_pair(): return lax.ppermute(block, 'grp', [(i, i ^ step) for i in range(n_grp)])  10.6 us
    ppermute x4, starting transfers between devices, from_pair(): return lax.ppermute(block, 'grp', [(i, i ^ step) for i in range(n_grp)])  6.58 us
    pallas_call x1, Pallas kernels, attend(): pl.pallas_call(attend_kernel, out_shape=near_out((n_tp, MSG_ROWS, LANES),...  4.07 us
  transfers between devices with their start and end apart: 6, of which 4 were waited for; matrix products, arithmetic and copies ran while one was open for 0% of the time, Pallas kernels for 0%

profile of v5, /device:TPU:1, one launch (start us, length us, event | category | flops | bytes accessed | tf_op | source)
XLA Modules:
  0.0 90.2 jit_solution(1394905861921152541)
XLA Ops:
  0.0 1.4 %copies.1 = bf16[32,16,128]{2,1,0:T(8,128)(2,1)} custom-call(bf16[16,128]{1,0:T(8,128)(2,1)} %bitcast.9), custom_call_target="tpu_custom_call" | custom-call | flops 99999997952 | bytes 135168 | tf_op jit(solution)/shard_map/copies/pallas_call | solution.py:298
  1.4 0.0 copy-start
  1.4 0.0 copy-start.1
  1.4 12.7 %all-to-all-start = ((bf16[32,16,128]{2,1,0:T(8,128)(2,1)}), bf16[32,16,128]{2,1,0:T(8,128)(2,1)S(1)}, u32[]{:S(2)}, u32[]{:S(2)}) async-start(bf16[32,16,128]{2,1,0:T(8,128)(2,1)} %copies.1), calls=%async_computation | async-start | bytes 262144 | tf_op jit(solution)/shard_map/all_to_all | solution.py:395
  14.7 9.9 %all-to-all-done.q_ref = bf16[32,16,128]{2,1,0:T(8,128)(2,1)S(1)} async-done(((bf16[32,16,128]{2,1,0:T(8,128)(2,1)}), bf16[32,16,128]{2,1,0:T(8,128)(2,1)S(1)}, u32[]{:S(2)}, u32[]{:S(2)}) %all-to-all-start) | async-done | bytes 131104 | tf_op jit(solution)/shard_map/all_to_all | solution.py:395
  24.6 4.1 %attend.1 = bf16[32,24,128]{2,1,0:T(8,128)(2,1)} custom-call(s32[1]{0:T(128)S(6)} %copy.8.size_ref, s32[16]{0:T(128)} %bitcast.13, s32[16,16]{1,0:T(8,128)} %bitcast.12, bf16[32,16,128]{2,1,0:T(8,128)(2,1)S(1)} %all-to-all-done.q_ref, bf16[256,16,1024]{2,1,0:T(8,128)(2,1)} %bitcast.11), custom_call_target="tpu_custom_call" | custom-call | tf_op jit(solution)/shard_map/attend/pallas_call | solution.py:326
  28.7 5.2 %all-to-all-start.1 = ((bf16[32,24,128]{2,1,0:T(8,128)(2,1)}), bf16[32,24,128]{2,1,0:T(8,128)(2,1)S(1)}, u32[]{:S(2)}, u32[]{:S(2)}) async-start(bf16[32,24,128]{2,1,0:T(8,128)(2,1)} %attend.1), calls=%async_computation.1 | async-start | bytes 393216 | tf_op jit(solution)/shard_map/all_to_all | solution.py:395
  33.9 0.0 copy-done
  33.9 0.2 collective-permute-start
  34.1 4.1 %collective-permute-done.other_ref = bf16[360,128]{1,0:T(8,128)(2,1)S(1)} collective-permute-done((bf16[360,128]{1,0:T(8,128)(2,1)S(1)}, bf16[360,128]{1,0:T(8,128)(2,1)S(1)}, u32[]{:S(2)}, u32[]{:S(2)}) %collective-permute-start) | collective-permute-done | bytes 92192 | tf_op jit(solution)/shard_map/ppermute | solution.py:405
  38.2 3.0 %collective-permute-start.3 = (bf16[720,128]{1,0:T(8,128)(2,1)S(1)}, bf16[720,128]{1,0:T(8,128)(2,1)S(1)}, u32[]{:S(2)}, u32[]{:S(2)}) collective-permute-start(bf16[720,128]{1,0:T(8,128)(2,1)S(1)} %join.1.rest_0_), channel_id=1, source_target_pairs={{0,32},{32,0},{64,96},{96,64},{128,160},{160,128},{192,224},{224,1... | collective-permute-start | bytes 552968 | tf_op jit(solution)/shard_map/ppermute | solution.py:405
  41.2 3.3 %collective-permute-start.2 = (bf16[720,128]{1,0:T(8,128)(2,1)S(1)}, bf16[720,128]{1,0:T(8,128)(2,1)S(1)}, u32[]{:S(2)}, u32[]{:S(2)}) collective-permute-start(bf16[720,128]{1,0:T(8,128)(2,1)S(1)} %join.1.rest_0_), channel_id=1, source_target_pairs={{0,96},{32,64},{64,32},{96,0},{128,224},{160,192},{192,160},{224,1... | collective-permute-start | bytes 552968 | tf_op jit(solution)/shard_map/ppermute | solution.py:405
  44.5 0.0 collective-permute-start.1
  44.5 1.1 %all-to-all-done.1.msg_ref = bf16[32,24,128]{2,1,0:T(8,128)(2,1)S(1)} async-done(((bf16[32,24,128]{2,1,0:T(8,128)(2,1)}), bf16[32,24,128]{2,1,0:T(8,128)(2,1)S(1)}, u32[]{:S(2)}, u32[]{:S(2)}) %all-to-all-start.1) | async-done | bytes 196640 | tf_op jit(solution)/shard_map/all_to_all | solution.py:395
  45.6 0.0 copy-done.1
  45.6 0.0 copy-done.2
  45.6 0.3 merge.1.attended_ref
  45.9 0.0 collective-permute-done.3.rest_3_
  45.9 6.6 %collective-permute-done.2.rest_2_ = bf16[720,128]{1,0:T(8,128)(2,1)S(1)} collective-permute-done((bf16[720,128]{1,0:T(8,128)(2,1)S(1)}, bf16[720,128]{1,0:T(8,128)(2,1)S(1)}, u32[]{:S(2)}, u32[]{:S(2)}) %collective-permute-start.2) | collective-permute-done | bytes 184352 | tf_op jit(solution)/shard_map/ppermute | solution.py:405
  52.5 0.0 collective-permute-done.1.rest_1_
  52.5 0.4 project.1
  52.9 22.3 %all_to_all.20.in_ref = bf16[32,4,384]{2,1,0:T(4,128)(2,1)S(1)} all-to-all(bf16[32,4,384]{2,1,0:T(4,128)(2,1)S(1)} %project.1), channel_id=1, replica_groups=mesh['grp'=8,'tp'=32] {'tp'}, dimensions={0} | all-to-all | bytes 196608 | tf_op jit(solution)/shard_map/all_to_all | solution.py:395
  75.2 14.2 %all_to_all.21.in_ref = bf16[32,4,384]{2,1,0:T(4,128)(2,1)S(1)} all-to-all(bf16[32,4,384]{2,1,0:T(4,128)(2,1)S(1)} %total.1), channel_id=1, replica_groups=mesh['grp'=8,'tp'=32] {'tp'}, dimensions={0} | all-to-all | bytes 196608 | tf_op jit(solution)/shard_map/all_to_all | solution.py:395
  89.4 0.8 finish.1
  (3 shorter events, 0.1 us)
Async XLA Ops:
  1.4 32.5 %copy-start = (bf16[128,360]{0,1:T(8,128)(2,1)S(1)}, bf16[128,360]{0,1:T(8,128)(2,1)}, u32[]{:S(2)}) copy-start(bf16[128,360]{0,1:T(8,128)(2,1)} %param.13) | copy-start | bytes 276484
  1.4 44.2 %copy-start.1 = (bf16[1,16,1024]{2,1,0:T(8,128)(2,1)S(1)}, bf16[1,16,1024]{2,1,0:T(8,128)(2,1)}, u32[]{:S(2)}) copy-start(bf16[1,16,1024]{2,1,0:T(8,128)(2,1)} %param.12) | copy-start | bytes 98308
  1.4 44.2 %copy-start.2 = (bf16[1,16,128]{2,1,0:T(8,128)(2,1)S(1)}, bf16[1,16,128]{2,1,0:T(8,128)(2,1)}, u32[]{:S(2)}) copy-start(bf16[1,16,128]{2,1,0:T(8,128)(2,1)} %param.10) | copy-start | bytes 12292
  1.4 23.2 %all-to-all-start = ((bf16[32,16,128]{2,1,0:T(8,128)(2,1)}), bf16[32,16,128]{2,1,0:T(8,128)(2,1)S(1)}, u32[]{:S(2)}, u32[]{:S(2)}) async-start(bf16[32,16,128]{2,1,0:T(8,128)(2,1)} %copies.1), calls=%async_computation | async-start | bytes 262144 | tf_op jit(solution)/shard_map/all_to_all | solution.py:395
  28.7 16.9 %all-to-all-start.1 = ((bf16[32,24,128]{2,1,0:T(8,128)(2,1)}), bf16[32,24,128]{2,1,0:T(8,128)(2,1)S(1)}, u32[]{:S(2)}, u32[]{:S(2)}) async-start(bf16[32,24,128]{2,1,0:T(8,128)(2,1)} %attend.1), calls=%async_computation.1 | async-start | bytes 393216 | tf_op jit(solution)/shard_map/all_to_all | solution.py:395
  33.9 4.3 %collective-permute-start = (bf16[360,128]{1,0:T(8,128)(2,1)S(1)}, bf16[360,128]{1,0:T(8,128)(2,1)S(1)}, u32[]{:S(2)}, u32[]{:S(2)}) collective-permute-start(bf16[360,128]{1,0:T(8,128)(2,1)S(1)} %bitcast.6), channel_id=1, source_target_pairs={{0,128},{32,160},{64,192},{96,224},{128,0},{160,32},{192,64},{224,... | collective-permute-start | bytes 276488 | tf_op jit(solution)/shard_map/ppermute | solution.py:405
  38.2 7.7 %collective-permute-start.3 = (bf16[720,128]{1,0:T(8,128)(2,1)S(1)}, bf16[720,128]{1,0:T(8,128)(2,1)S(1)}, u32[]{:S(2)}, u32[]{:S(2)}) collective-permute-start(bf16[720,128]{1,0:T(8,128)(2,1)S(1)} %join.1.rest_0_), channel_id=1, source_target_pairs={{0,32},{32,0},{64,96},{96,64},{128,160},{160,128},{192,224},{224,1... | collective-permute-start | bytes 552968 | tf_op jit(solution)/shard_map/ppermute | solution.py:405
  41.2 11.3 %collective-permute-start.2 = (bf16[720,128]{1,0:T(8,128)(2,1)S(1)}, bf16[720,128]{1,0:T(8,128)(2,1)S(1)}, u32[]{:S(2)}, u32[]{:S(2)}) collective-permute-start(bf16[720,128]{1,0:T(8,128)(2,1)S(1)} %join.1.rest_0_), channel_id=1, source_target_pairs={{0,96},{32,64},{64,32},{96,0},{128,224},{160,192},{192,160},{224,1... | collective-permute-start | bytes 552968 | tf_op jit(solution)/shard_map/ppermute | solution.py:405
  44.5 8.0 %collective-permute-start.1 = (bf16[720,128]{1,0:T(8,128)(2,1)S(1)}, bf16[720,128]{1,0:T(8,128)(2,1)S(1)}, u32[]{:S(2)}, u32[]{:S(2)}) collective-permute-start(bf16[720,128]{1,0:T(8,128)(2,1)S(1)} %join.1.rest_0_), channel_id=1, source_target_pairs={{0,64},{32,96},{64,0},{96,32},{128,192},{160,224},{192,128},{224,1... | collective-permute-start | bytes 552968 | tf_op jit(solution)/shard_map/ppermute | solution.py:405

commit v6 on v5

--- a/solution.py
+++ b/solution.py
@@ -15,8 +15,7 @@
 NEG_BIG = -1e30
 BF = jnp.bfloat16
 F32 = jnp.float32
-STAT_ROW = 16
-MSG_ROWS = 24
+ROWS = 2
 INTERPRET = False
 FIRST_STEP = 4
 PAIR_STEPS = (2, 3, 1)
@@ -161,13 +160,15 @@
     packed = tops + roll_lanes(hi.astype(F32), slots) + roll_lanes(lo.astype(F32), 2 * slots)
     stat_scr[...] = packed[:n_tp] + roll_lanes(packed[n_tp:], HD)
     for t in range(n_tp):
-        out_ref[t, 0:slots, :] = num_scr[pl.ds(t, slots, stride=n_tp + 1), :].astype(BF)
-        out_ref[t, STAT_ROW:MSG_ROWS, :] = jnp.broadcast_to(
-            stat_scr[t : t + 1, :], (MSG_ROWS - STAT_ROW, LANES)
+        for i in range(slots // ROWS):
+            pick = pl.ds(i * ROWS * (n_tp + 1) + t, ROWS, stride=n_tp + 1)
+            out_ref[t, :, i * LANES : (i + 1) * LANES] = num_scr[pick, :].astype(BF)
+        out_ref[t, :, slots // ROWS * LANES :] = jnp.broadcast_to(
+            stat_scr[t : t + 1, :], (ROWS, LANES)
         ).astype(BF)
 
 
-def merge_kernel(size_ref, msg_ref, q_ref, new_ref, out_ref):
+def merge_kernel(size_ref, msg_ref, q_ref, new_ref, out_ref, msg_scr):
     n_tp = msg_ref.shape[0]
     slots = q_ref.shape[0]
     live_count = size_ref[0]
@@ -176,8 +177,15 @@
         lax.broadcasted_iota(jnp.int32, (LANES, LANES), 0) // HD
         == lax.broadcasted_iota(jnp.int32, (LANES, LANES), 1) // HD
     ).astype(F32).astype(BF)
-    rows8 = MSG_ROWS - STAT_ROW
-    stats = [msg_ref[t, STAT_ROW:MSG_ROWS, :].astype(F32) for t in range(n_tp)]
+    rows8 = 8
+    stats = []
+    for t in range(n_tp):
+        for i in range(slots // ROWS):
+            msg_scr[t * slots + i * ROWS : t * slots + (i + 1) * ROWS, :] = msg_ref[
+                t, :, i * LANES : (i + 1) * LANES
+            ].astype(F32)
+        stat = msg_ref[t, :, slots // ROWS * LANES :].astype(F32)
+        stats.append(jnp.broadcast_to(stat[0:1], (rows8, LANES)))
     top = functools.reduce(jnp.maximum, stats)
     scale = [jnp.exp(s - top) for s in stats]
     sums = sum(
@@ -197,7 +205,7 @@
     top_all = spread[n_tp * slots : (n_tp + 1) * slots]
     sum_all = spread[(n_tp + 1) * slots :]
     numerator = sum(
-        msg_ref[t, 0:slots, :].astype(F32) * spread[t * slots : (t + 1) * slots]
+        msg_scr[t * slots : (t + 1) * slots, :] * spread[t * slots : (t + 1) * slots]
         for t in range(n_tp)
     )
 
@@ -325,7 +333,7 @@
     n_tp, slots, _ = gathered.shape
     return pl.pallas_call(
         attend_kernel,
-        out_shape=near_out((n_tp, MSG_ROWS, LANES), BF),
+        out_shape=near_out((n_tp, ROWS, (slots // ROWS + 1) * LANES), BF),
         in_specs=[SMEM(), SMEM(), SMEM(), VMEM(), pl.BlockSpec(memory_space=pltpu.HBM)],
         out_specs=VMEM(),
         scratch_shapes=[
@@ -338,7 +346,7 @@
         interpret=bool(INTERPRET),
         compiler_params=PARAMS,
         name="attend",
-    )(sizes, far(lens), far(table), near(gathered), far(pool))
+    )(sizes, near(lens), near(table), near(gathered), far(pool))
 
 
 def merge(sizes, message, own, fresh):
@@ -347,6 +355,7 @@
         out_shape=near_out(own.shape, BF),
         in_specs=[SMEM()] + [VMEM()] * 3,
         out_specs=VMEM(),
+        scratch_shapes=[pltpu.VMEM((message.shape[0] * own.shape[0] + 8, LANES), F32)],
         interpret=bool(INTERPRET),
         compiler_params=PARAMS,
         name="merge",

time: 90.7 us -> 90.4 us (level)
  no operation moved by 1% of the time
where the time goes in v6:
time: 90.4 us; the launch traced here: 89.9 us
  blocking collectives  36.5 us (40%)
  starting transfers between devices  24.2 us (27%)
  waiting for transfers between devices  21.6 us (24%)
  Pallas kernels  6.9 us (8%)
    all_to_all x2, blocking collectives, exchange(): return lax.all_to_all(pieces, axis, split_axis=0, concat_axis=0, tiled=True)  36.5 us
    all_to_all x2, starting transfers between devices, exchange(): return lax.all_to_all(pieces, axis, split_axis=0, concat_axis=0, tiled=True)  17.9 us
    ppermute x4, waiting for transfers between devices, from_pair(): return lax.ppermute(block, 'grp', [(i, i ^ step) for i in range(n_grp)])  11.4 us
    all_to_all x2, waiting for transfers between devices, exchange(): return lax.all_to_all(pieces, axis, split_axis=0, concat_axis=0, tiled=True)  10.2 us
    ppermute x4, starting transfers between devices, from_pair(): return lax.ppermute(block, 'grp', [(i, i ^ step) for i in range(n_grp)])  6.3 us
    pallas_call x1, Pallas kernels, attend(): pl.pallas_call(attend_kernel, out_shape=near_out((n_tp, ROWS, (slots // R...  3.95 us
  transfers between devices with their start and end apart: 6, of which 4 were waited for; matrix products, arithmetic and copies ran while one was open for 0% of the time, Pallas kernels for 0%

profile of v6, /device:TPU:1, one launch (start us, length us, event | category | flops | bytes accessed | tf_op | source)
XLA Modules:
  0.0 89.9 jit_solution(3127200962697728260)
XLA Ops:
  0.0 1.4 %copies.1 = bf16[32,16,128]{2,1,0:T(8,128)(2,1)} custom-call(bf16[16,128]{1,0:T(8,128)(2,1)} %bitcast.10), custom_call_target="tpu_custom_call" | custom-call | flops 99999997952 | bytes 135168 | tf_op jit(solution)/shard_map/copies/pallas_call | solution.py:306
  1.4 12.7 %all-to-all-start = ((bf16[32,16,128]{2,1,0:T(8,128)(2,1)}), bf16[32,16,128]{2,1,0:T(8,128)(2,1)S(1)}, u32[]{:S(2)}, u32[]{:S(2)}) async-start(bf16[32,16,128]{2,1,0:T(8,128)(2,1)} %copies.1), calls=%async_computation | async-start | bytes 262144 | tf_op jit(solution)/shard_map/all_to_all | solution.py:404
  14.8 9.9 %all-to-all-done.q_ref = bf16[32,16,128]{2,1,0:T(8,128)(2,1)S(1)} async-done(((bf16[32,16,128]{2,1,0:T(8,128)(2,1)}), bf16[32,16,128]{2,1,0:T(8,128)(2,1)S(1)}, u32[]{:S(2)}, u32[]{:S(2)}) %all-to-all-start) | async-done | bytes 131104 | tf_op jit(solution)/shard_map/all_to_all | solution.py:404
  24.6 0.0 copy-done.2
  24.6 0.0 copy-done.4
  24.6 4.0 %attend.1 = bf16[32,2,1152]{2,1,0:T(2,128)(2,1)} custom-call(s32[1]{0:T(128)S(6)} %copy.8.size_ref, s32[16]{0:T(128)S(1)} %bitcast.12, s32[16,16]{1,0:T(8,128)S(1)} %bitcast.9, bf16[32,16,128]{2,1,0:T(8,128)(2,1)S(1)} %all-to-all-done.q_ref, bf16[256,16,1024]{2,1,0:T(8,128)(2,1)} %bitcast.13), custom_call_target="tpu_custom_call" | custom-call | tf_op jit(solution)/shard_map/attend/pallas_call | solution.py:334
  28.6 5.2 %all-to-all-start.1 = ((bf16[32,2,1152]{2,1,0:T(2,128)(2,1)}), bf16[32,2,1152]{2,1,0:T(2,128)(2,1)S(1)}, u32[]{:S(2)}, u32[]{:S(2)}) async-start(bf16[32,2,1152]{2,1,0:T(2,128)(2,1)} %attend.1), calls=%async_computation.1 | async-start | bytes 294912 | tf_op jit(solution)/shard_map/all_to_all | solution.py:404
  33.8 0.0 copy-done
  33.8 0.2 collective-permute-start
  34.0 4.2 %collective-permute-done.other_ref = bf16[360,128]{1,0:T(8,128)(2,1)S(1)} collective-permute-done((bf16[360,128]{1,0:T(8,128)(2,1)S(1)}, bf16[360,128]{1,0:T(8,128)(2,1)S(1)}, u32[]{:S(2)}, u32[]{:S(2)}) %collective-permute-start) | collective-permute-done | bytes 92192 | tf_op jit(solution)/shard_map/ppermute | solution.py:414
  38.2 2.8 %collective-permute-start.3 = (bf16[720,128]{1,0:T(8,128)(2,1)S(1)}, bf16[720,128]{1,0:T(8,128)(2,1)S(1)}, u32[]{:S(2)}, u32[]{:S(2)}) collective-permute-start(bf16[720,128]{1,0:T(8,128)(2,1)S(1)} %join.1.rest_0_), channel_id=1, source_target_pairs={{0,32},{32,0},{64,96},{96,64},{128,160},{160,128},{192,224},{224,1... | collective-permute-start | bytes 552968 | tf_op jit(solution)/shard_map/ppermute | solution.py:414
  41.0 3.3 %collective-permute-start.2 = (bf16[720,128]{1,0:T(8,128)(2,1)S(1)}, bf16[720,128]{1,0:T(8,128)(2,1)S(1)}, u32[]{:S(2)}, u32[]{:S(2)}) collective-permute-start(bf16[720,128]{1,0:T(8,128)(2,1)S(1)} %join.1.rest_0_), channel_id=1, source_target_pairs={{0,96},{32,64},{64,32},{96,0},{128,224},{160,192},{192,160},{224,1... | collective-permute-start | bytes 552968 | tf_op jit(solution)/shard_map/ppermute | solution.py:414
  44.3 0.0 collective-permute-start.1
  44.3 0.4 all-to-all-done.1.msg_ref
  44.7 0.0 copy-done.1
  44.7 0.0 copy-done.3
  44.7 0.4 merge.1.attended_ref
  45.0 0.0 collective-permute-done.3.rest_3_
  45.1 7.2 %collective-permute-done.2.rest_2_ = bf16[720,128]{1,0:T(8,128)(2,1)S(1)} collective-permute-done((bf16[720,128]{1,0:T(8,128)(2,1)S(1)}, bf16[720,128]{1,0:T(8,128)(2,1)S(1)}, u32[]{:S(2)}, u32[]{:S(2)}) %collective-permute-start.2) | collective-permute-done | bytes 184352 | tf_op jit(solution)/shard_map/ppermute | solution.py:414
  52.2 0.0 collective-permute-done.1.rest_1_
  52.2 0.4 project.1
  52.6 22.3 %all_to_all.20.in_ref = bf16[32,4,384]{2,1,0:T(4,128)(2,1)S(1)} all-to-all(bf16[32,4,384]{2,1,0:T(4,128)(2,1)S(1)} %project.1), channel_id=1, replica_groups=mesh['grp'=8,'tp'=32] {'tp'}, dimensions={0} | all-to-all | bytes 196608 | tf_op jit(solution)/shard_map/all_to_all | solution.py:404
  74.9 14.2 %all_to_all.21.in_ref = bf16[32,4,384]{2,1,0:T(4,128)(2,1)S(1)} all-to-all(bf16[32,4,384]{2,1,0:T(4,128)(2,1)S(1)} %total.1), channel_id=1, replica_groups=mesh['grp'=8,'tp'=32] {'tp'}, dimensions={0} | all-to-all | bytes 196608 | tf_op jit(solution)/shard_map/all_to_all | solution.py:404
  89.1 0.8 finish.1
  (7 shorter events, 0.1 us)
Async XLA Ops:
  0.0 24.6 %copy-start.2 = (s32[1,16,16]{2,1,0:T(8,128)S(1)}, s32[1,16,16]{2,1,0:T(8,128)}, u32[]{:S(2)}) copy-start(s32[1,16,16]{2,1,0:T(8,128)} %param.9) | copy-start | bytes 3076
  0.0 24.6 %copy-start.4 = (s32[1,16]{1,0:T(1,128)S(1)}, s32[1,16]{1,0:T(1,128)}, u32[]{:S(2)}) copy-start(s32[1,16]{1,0:T(1,128)} %param.8) | copy-start | bytes 196
  1.4 32.4 %copy-start = (bf16[128,360]{0,1:T(8,128)(2,1)S(1)}, bf16[128,360]{0,1:T(8,128)(2,1)}, u32[]{:S(2)}) copy-start(bf16[128,360]{0,1:T(8,128)(2,1)} %param.13) | copy-start | bytes 276484
  1.4 43.3 %copy-start.1 = (bf16[1,16,1024]{2,1,0:T(8,128)(2,1)S(1)}, bf16[1,16,1024]{2,1,0:T(8,128)(2,1)}, u32[]{:S(2)}) copy-start(bf16[1,16,1024]{2,1,0:T(8,128)(2,1)} %param.12) | copy-start | bytes 98308
  1.4 43.3 %copy-start.3 = (bf16[1,16,128]{2,1,0:T(8,128)(2,1)S(1)}, bf16[1,16,128]{2,1,0:T(8,128)(2,1)}, u32[]{:S(2)}) copy-start(bf16[1,16,128]{2,1,0:T(8,128)(2,1)} %param.10) | copy-start | bytes 12292
  1.4 23.2 %all-to-all-start = ((bf16[32,16,128]{2,1,0:T(8,128)(2,1)}), bf16[32,16,128]{2,1,0:T(8,128)(2,1)S(1)}, u32[]{:S(2)}, u32[]{:S(2)}) async-start(bf16[32,16,128]{2,1,0:T(8,128)(2,1)} %copies.1), calls=%async_computation | async-start | bytes 262144 | tf_op jit(solution)/shard_map/all_to_all | solution.py:404
  28.6 16.1 %all-to-all-start.1 = ((bf16[32,2,1152]{2,1,0:T(2,128)(2,1)}), bf16[32,2,1152]{2,1,0:T(2,128)(2,1)S(1)}, u32[]{:S(2)}, u32[]{:S(2)}) async-start(bf16[32,2,1152]{2,1,0:T(2,128)(2,1)} %attend.1), calls=%async_computation.1 | async-start | bytes 294912 | tf_op jit(solution)/shard_map/all_to_all | solution.py:404
  33.8 4.4 %collective-permute-start = (bf16[360,128]{1,0:T(8,128)(2,1)S(1)}, bf16[360,128]{1,0:T(8,128)(2,1)S(1)}, u32[]{:S(2)}, u32[]{:S(2)}) collective-permute-start(bf16[360,128]{1,0:T(8,128)(2,1)S(1)} %bitcast.6), channel_id=1, source_target_pairs={{0,128},{32,160},{64,192},{96,224},{128,0},{160,32},{192,64},{224,... | collective-permute-start | bytes 276488 | tf_op jit(solution)/shard_map/ppermute | solution.py:414
  38.2 6.8 %collective-permute-start.3 = (bf16[720,128]{1,0:T(8,128)(2,1)S(1)}, bf16[720,128]{1,0:T(8,128)(2,1)S(1)}, u32[]{:S(2)}, u32[]{:S(2)}) collective-permute-start(bf16[720,128]{1,0:T(8,128)(2,1)S(1)} %join.1.rest_0_), channel_id=1, source_target_pairs={{0,32},{32,0},{64,96},{96,64},{128,160},{160,128},{192,224},{224,1... | collective-permute-start | bytes 552968 | tf_op jit(solution)/shard_map/ppermute | solution.py:414
  41.0 11.2 %collective-permute-start.2 = (bf16[720,128]{1,0:T(8,128)(2,1)S(1)}, bf16[720,128]{1,0:T(8,128)(2,1)S(1)}, u32[]{:S(2)}, u32[]{:S(2)}) collective-permute-start(bf16[720,128]{1,0:T(8,128)(2,1)S(1)} %join.1.rest_0_), channel_id=1, source_target_pairs={{0,96},{32,64},{64,32},{96,0},{128,224},{160,192},{192,160},{224,1... | collective-permute-start | bytes 552968 | tf_op jit(solution)/shard_map/ppermute | solution.py:414
  44.3 7.9 %collective-permute-start.1 = (bf16[720,128]{1,0:T(8,128)(2,1)S(1)}, bf16[720,128]{1,0:T(8,128)(2,1)S(1)}, u32[]{:S(2)}, u32[]{:S(2)}) collective-permute-start(bf16[720,128]{1,0:T(8,128)(2,1)S(1)} %join.1.rest_0_), channel_id=1, source_target_pairs={{0,64},{32,96},{64,0},{96,32},{128,192},{160,224},{192,128},{224,1... | collective-permute-start | bytes 552968 | tf_op jit(solution)/shard_map/ppermute | solution.py:414
